TPU v7x, 32 devices: a whole 2x2x4 slice. The times are simulated.
32 devices in a mesh: batch: 2 (over x), col: 4 (over z), row: 4 (over y, core).
Axes of the slice: x: 2, y: 2, z: 4, core: 2. Of those that a mesh axis runs over, the one named last changes fastest.
Arguments:
- pair_rep: bfloat16 [1536, 768, 64], P(('batch', 'row'), 'col'), parts along dimension 0
- pair_mask: int32 [1536, 768], P(('batch', 'row'), 'col'), parts along dimension 0
- ln_in_scale: bfloat16 [64], replicated
- w_left: bfloat16 [64, 64], replicated
- w_left_gate: bfloat16 [64, 64], replicated
- w_right: bfloat16 [64, 64], replicated
- w_right_gate: bfloat16 [64, 64], replicated
- w_out_gate: bfloat16 [64, 64], replicated
- ln_out_scale: bfloat16 [64], replicated
- w_out: bfloat16 [64, 64], replicated
Outputs:
- output: bfloat16 [1536, 768, 64], P(('batch', 'row'), 'col'), parts along dimension 0
There are 2 independent parts. A program takes and returns all parts, laid end to end along the dimension named above; an argument that names none is the same for every part.
All inputs are finite; a program needn't handle non-finite values.
Results may differ from a plain program's by a relative error of at most 0.001.
Values are sent between devices in bfloat16 or wider.
A program may use at most 1 GiB of HBM per device.

v0:
```python
import jax
import jax.numpy as jnp
from jax import lax
from jax.sharding import PartitionSpec as P

LN_EPS = 0.00001


def layer_norm(values, gain_vec):
    mean_val = jnp.mean(values, axis=-1, keepdims=True)
    centered = values - mean_val
    variance = jnp.mean(centered * centered, axis=-1, keepdims=True)
    return centered * lax.rsqrt(variance + LN_EPS) * gain_vec.astype(jnp.float32)


def project_tile(pair_tile, mask_tile, ln_in_scale, w_left, w_left_gate, w_right, w_right_gate, w_out_gate):
    tri_dim = w_left.shape[1]
    normed = layer_norm(pair_tile.astype(jnp.float32), ln_in_scale).astype(jnp.bfloat16)
    w_cat = jnp.concatenate([w_left, w_left_gate, w_right, w_right_gate, w_out_gate], axis=1)
    proj_all = jnp.einsum('ijz,zh->ijh', normed, w_cat, preferred_element_type=jnp.float32)
    keep_mask = mask_tile.astype(jnp.float32)[:, :, None]
    left_act = (keep_mask * jax.nn.sigmoid(proj_all[:, :, tri_dim:2 * tri_dim]) * proj_all[:, :, :tri_dim]).astype(jnp.bfloat16)
    right_act = (keep_mask * jax.nn.sigmoid(proj_all[:, :, 3 * tri_dim:4 * tri_dim]) * proj_all[:, :, 2 * tri_dim:3 * tri_dim]).astype(jnp.bfloat16)
    gate_act = jax.nn.sigmoid(proj_all[:, :, 4 * tri_dim:])
    return left_act, right_act, gate_act


def finish_tile(normed_out, pair_tile, gate_act, w_out):
    update = jnp.einsum('ijh,hz->ijz', normed_out, w_out, preferred_element_type=jnp.float32)
    return (pair_tile.astype(jnp.float32) + gate_act * update).astype(jnp.bfloat16)


def solution(mesh):
    row_count = mesh.shape['row']
    col_count = mesh.shape['col']
    tile_spec = P(('batch', 'row'), 'col', None)
    mask_spec = P(('batch', 'row'), 'col')
    replicated = P()

    def local_step(pair_tile, mask_tile, ln_in_scale, w_left, w_left_gate, w_right, w_right_gate, w_out_gate, ln_out_scale, w_out):
        left_act, right_act, gate_act = project_tile(pair_tile, mask_tile, ln_in_scale, w_left, w_left_gate, w_right, w_right_gate, w_out_gate)
        tile_rows, tile_cols, tri_dim = left_act.shape
        sub_len = tile_rows // col_count
        moved_a = lax.all_to_all(left_act, 'col', 0, 1, tiled=True)
        moved_a = lax.all_to_all(moved_a, 'row', 1, 0, tiled=True)
        left_panel = lax.all_gather(moved_a, 'col', axis=0, tiled=True).reshape(col_count, row_count, sub_len, tile_rows, tri_dim)
        right_panel = lax.all_gather(right_act, 'row', axis=0, tiled=True).reshape(row_count, col_count, sub_len, tile_cols, tri_dim)
        summed = jnp.einsum('ursih,rusjh->ijh', left_panel, right_panel, preferred_element_type=jnp.float32)
        normed_out = layer_norm(summed, ln_out_scale).astype(jnp.bfloat16)
        return finish_tile(normed_out, pair_tile, gate_act, w_out)

    return jax.shard_map(local_step, mesh=mesh, in_specs=(tile_spec, mask_spec) + (replicated,) * 8, out_specs=tile_spec, check_vma=False)
```

profile of v0, /device:TPU:16, one launch (start us, length us, event | category | flops | bytes accessed | tf_op | source)
XLA Modules:
  0.0 896.7 jit_solution(772940183037542010)
XLA Ops:
  6.6 5.2 convert_reduce_fusion
  11.9 5.9 fusion.5
  17.9 0.1 concatenate.3
  18.0 24.8 %fusion.23 = f32[192,192,320]{1,2,0:T(8,128)} fusion(bf16[192,192,64]{1,2,0:T(8,128)(2,1)} %param.10, f32[64]{0:T(128)S(1)} %convert_element_type.29, f32[192,192]{1,0:T(8,128)S(1)} %add_rsqrt_fusion.1, f32[192,192]{1,0:T(8,128)S(1)} %broadcast_multiply_fusion.1, bf16[64,320]{1,0:T(8,128)(2,1)S(1)} %concatenate.3), kind=kOutput, calls=%fused_computation.35 | convolution fusion | flops 1521745920 | bytes 52240640 | tf_op jit(solution)/shard_map/ijz,zh->ijh/dot_general | solution.py:20
  42.9 23.4 %fusion.14 = (bf16[192,192,64]{1,2,0:T(8,128)(2,1)}, bf16[192,192,64]{1,2,0:T(8,128)(2,1)}) fusion(f32[192,192,320]{1,2,0:T(8,128)} %fusion.23, f32[192,192]{1,0:T(8,128)S(1)} %convert_element_type.31), kind=kLoop, calls=%fused_computation.20 | loop fusion | flops 28311552 | bytes 47333376 | tf_op jit(solution)/shard_map/convert_element_type | solution.py:23
  66.3 0.0 all-gather.5.cloned.1.call-start
  66.4 140.5 %all_to_all.36 = bf16[192,192,64]{1,2,0:T(8,128)(2,1)S(1)} all-to-all(bf16[192,192,64]{1,2,0:T(8,128)(2,1)} %get-tuple-element.6), channel_id=1, replica_groups=mesh['batch'=2,'col'=4,'row'=4] {'col'}, dimensions={0} | all-to-all | bytes 9437184 | tf_op jit(solution)/shard_map/all_to_all | solution.py:44
  206.9 8.8 copy.131
  215.7 13.7 %copy.117 = bf16[48,4,192,64]{3,0,2,1:T(8,128)(2,1)} copy(bf16[48,4,192,64]{2,1,3,0:T(4,128)(2,1)} %bitcast.34) | data formatting | bytes 9437184 | tf_op jit(solution)/shard_map/all_to_all | solution.py:44
  229.3 10.4 %reshape.38 = bf16[4,2,294912]{2,1,0:T(2,128)(2,1)} reshape(bf16[768,48,64]{2,1,0:T(8,128)(2,1)} %bitcast.30) | data formatting | bytes 9437184
  239.7 59.4 %all_to_all.37 = bf16[4,2,294912]{2,1,0:T(2,128)(2,1)} all-to-all(bf16[4,2,294912]{2,1,0:T(2,128)(2,1)} %reshape.38), channel_id=1, replica_groups=mesh['batch'=2,'col'=4,'row'=4] {'row'}, dimensions={0} | all-to-all | bytes 9437184 | tf_op jit(solution)/shard_map/all_to_all | solution.py:45
  299.1 10.3 %reshape.39 = bf16[768,48,64]{2,1,0:T(8,128)(2,1)} reshape(bf16[4,2,294912]{2,1,0:T(2,128)(2,1)} %all_to_all.37) | data formatting | bytes 9437184
  309.4 14.7 %copy.118 = bf16[48,4,192,64]{2,1,3,0:T(4,128)(2,1)} copy(bf16[48,4,192,64]{3,0,2,1:T(8,128)(2,1)} %bitcast.31) | data formatting | bytes 9437184 | tf_op jit(solution)/shard_map/all_to_all | solution.py:45
  324.1 6.6 copy.105
  330.7 424.8 %all-gather.5.cloned.1.call-done = bf16[768,192,64]{1,2,0:T(8,128)(2,1)} async-done(((bf16[192,192,64]{1,2,0:T(8,128)(2,1)}), bf16[768,192,64]{1,2,0:T(8,128)(2,1)}) %all-gather.5.cloned.1.call-update) | async-done | bytes 18874384 | tf_op jit(solution)/shard_map/all_gather | solution.py:46
  755.5 95.6 %bitcast_reduce_fusion = (f32[192,192]{0,1:T(8,128)S(1)}, f32[64,192,192,1,1]{2,1,4,3,0:T(8,128)}) fusion(bf16[4,4,48,192,64]{3,4,2,1,0:T(8,128)(2,1)} %bitcast.37, bf16[4,4,48,192,64]{3,4,2,1,0:T(8,128)(2,1)} %bitcast.36), kind=kOutput, calls=%fused_computation.32 | convolution fusion | flops 3626201088 | bytes 47333376 | tf_op jit(solution)/shard_map/ursih,rusjh->ijh/dot_general | solution.py:48
  851.1 0.1 copy.108
  851.2 0.1 copy.109
  851.3 6.0 multiply_reduce_fusion
  857.4 0.1 copy.110
  857.5 0.1 copy.111
  857.7 9.4 %multiply_convert_fusion = bf16[192,192,64]{0,1,2:T(8,128)(2,1)} fusion(f32[64,192,192,1,1]{2,1,4,3,0:T(8,128)} %get-tuple-element.8, f32[64]{0:T(128)S(1)} %convert_element_type.34, f32[192,192]{0,1:T(8,128)S(1)} %copy.111, f32[192,192]{0,1:T(8,128)S(1)} %copy.109), kind=kLoop, calls=%fused_computation.33 | loop fusion | flops 9437184 | bytes 14450944 | tf_op jit(solution)/shard_map/convert_element_type | solution.py:49
  867.0 9.8 %copy.112 = bf16[192,192,64]{1,2,0:T(8,128)(2,1)} copy(bf16[192,192,64]{0,1,2:T(8,128)(2,1)} %multiply_convert_fusion) | data formatting | bytes 9437184 | tf_op jit(solution)/shard_map/convert_element_type | solution.py:49
  876.8 12.7 %fusion.8 = bf16[192,192,64]{1,2,0:T(8,128)(2,1)} fusion(bf16[192,192,64]{1,2,0:T(8,128)(2,1)} %param.10, f32[192,192,320]{1,2,0:T(8,128)} %fusion.23, bf16[192,192,64]{1,2,0:T(8,128)(2,1)} %copy.112, bf16[64,64]{1,0:T(8,128)(2,1)S(1)} %copy-done), kind=kOutput, calls=%fused_computation.11 | convolution fusion | flops 318504960 | bytes 23601152 | tf_op jit(solution)/shard_map/ijh,hz->ijz/dot_general | solution.py:29
  (29 shorter events, 0.3 us)
Async XLA Ops:
  6.5 870.3 %copy-start = (bf16[64,64]{1,0:T(8,128)(2,1)S(1)}, bf16[64,64]{1,0:T(8,128)(2,1)}, u32[]{:S(2)}) copy-start(bf16[64,64]{1,0:T(8,128)(2,1)} %param.19) | copy-start | bytes 24580
  6.5 11.3 %copy-start.7 = (bf16[64]{0:T(256)(128)(2,1)S(1)}, bf16[64]{0:T(256)(128)(2,1)}, u32[]{:S(2)}) copy-start(bf16[64]{0:T(256)(128)(2,1)} %param.12) | copy-start | bytes 388
  6.5 11.3 %copy-start.1 = (s32[192,192]{1,0:T(8,128)S(1)}, s32[192,192]{1,0:T(8,128)}, u32[]{:S(2)}) copy-start(s32[192,192]{1,0:T(8,128)} %param.11) | copy-start | bytes 442372
  6.5 11.3 %copy-start.2 = (bf16[64,64]{1,0:T(8,128)(2,1)S(1)}, bf16[64,64]{1,0:T(8,128)(2,1)}, u32[]{:S(2)}) copy-start(bf16[64,64]{1,0:T(8,128)(2,1)} %param.13) | copy-start | bytes 24580
  6.5 11.3 %copy-start.3 = (bf16[64,64]{1,0:T(8,128)(2,1)S(1)}, bf16[64,64]{1,0:T(8,128)(2,1)}, u32[]{:S(2)}) copy-start(bf16[64,64]{1,0:T(8,128)(2,1)} %param.14) | copy-start | bytes 24580
  6.5 11.3 %copy-start.4 = (bf16[64,64]{1,0:T(8,128)(2,1)S(1)}, bf16[64,64]{1,0:T(8,128)(2,1)}, u32[]{:S(2)}) copy-start(bf16[64,64]{1,0:T(8,128)(2,1)} %param.15) | copy-start | bytes 24580
  6.6 11.3 %copy-start.5 = (bf16[64,64]{1,0:T(8,128)(2,1)S(1)}, bf16[64,64]{1,0:T(8,128)(2,1)}, u32[]{:S(2)}) copy-start(bf16[64,64]{1,0:T(8,128)(2,1)} %param.16) | copy-start | bytes 24580
  6.6 11.3 %copy-start.6 = (bf16[64,64]{1,0:T(8,128)(2,1)S(1)}, bf16[64,64]{1,0:T(8,128)(2,1)}, u32[]{:S(2)}) copy-start(bf16[64,64]{1,0:T(8,128)(2,1)} %param.17) | copy-start | bytes 24580
  6.6 324.1 %all-gather.3.cloned.1.call-start = ((), (), s32[]{:S(2)}) async-start(), calls=%async_computation.2 | async-start | bytes 31457280 | tf_op jit(solution)/shard_map/all_gather | solution.py:47
  66.3 689.2 %all-gather.5.cloned.1.call-start = ((), (), s32[]{:S(2)}) async-start(), calls=%async_computation.3 | async-start | bytes 31457280 | tf_op jit(solution)/shard_map/all_gather | solution.py:46
  324.1 6.6 copy-start.8
Sparse Core Ops, SparseCore 0:
  66.4 156.6 all-gather.2
  330.8 424.7 all-gather.4
where the time goes:
time: 910 us; the launch traced here: 897 us
  waiting for transfers between devices  425 us (47%)
  blocking collectives  200 us (22%)
  matrix products  133 us (15%)
  local copies, waits for them, and re-layouts  74.7 us (8%)
  other arithmetic  50.1 us (6%)
  between operations  14 us (2%)
    all_gather x1, waiting for transfers between devices, local_step(): lax.all_gather(moved_a, 'col', axis=0, tiled=True)  425 us
    all_to_all x1, blocking collectives, local_step(): moved_a = lax.all_to_all(left_act, 'col', 0, 1, tiled=True)  141 us
    dot_general x1, matrix products, local_step(): jnp.einsum('ursih,rusjh->ijh', left_panel, right_panel, preferred_element...  95.6 us
    all_to_all x1, blocking collectives, local_step(): moved_a = lax.all_to_all(moved_a, 'row', 1, 0, tiled=True)  59.4 us
    dot_general x1, matrix products, project_tile(): jnp.einsum('ijz,zh->ijh', normed, w_cat, preferred_element_type=jnp.float32)  24.8 us
    convert_element_type x1, other arithmetic, project_tile(): (keep_mask * jax.nn.sigmoid(proj_all[:, :, 3 * tri_dim:4 * tri_dim]) * pr...  23.4 us
    all_to_all x2, local copies, waits for them, and re-layouts, local_step(): moved_a = lax.all_to_all(left_act, 'col', 0, 1, tiled=True)  22.4 us
    all_to_all x2, local copies, waits for them, and re-layouts, local_step(): moved_a = lax.all_to_all(moved_a, 'row', 1, 0, tiled=True)  21.2 us
  transfers between devices with their start and end apart: 2, of which 1 were waited for; matrix products, arithmetic and copies ran while one was open for 7% of the time, Pallas kernels for 0%

commit v1 on v0

v1 whole, which is shorter than its diff:
```python
import jax
import jax.numpy as jnp
from jax import lax
from jax.experimental import pallas as pl
from jax.experimental.pallas import tpu as pltpu
from jax.sharding import PartitionSpec as P

LN_EPS = 0.00001
MESH = pl.DeviceIdType.MESH
CHUNKS = 8


def sigmoid(v):
    return 0.5 * jnp.tanh(0.5 * v) + 0.5


def norm_channels(v, gain, axis):
    mean = jnp.mean(v, axis=axis, keepdims=True)
    cen = v - mean
    var = jnp.mean(cen * cen, axis=axis, keepdims=True)
    return cen * lax.rsqrt(var + LN_EPS) * gain


def project_kernel(z_ref, m_ref, gin_ref, we_ref, wo_ref, a_ref, b_ref):
    gain = gin_ref[...][None]
    for half in range(2):
        z = z_ref[16 * half:16 * half + 16].astype(jnp.float32)
        x = norm_channels(z, gain, 1).astype(jnp.bfloat16).reshape(4, 256, 192)
        m = m_ref[16 * half:16 * half + 16].astype(jnp.float32)

        def lanes(p, q):
            return jnp.concatenate([p[:, :128], q[:, :128], p[:, 128:], q[:, 128:]], axis=1)

        acts = []
        for par, w_ref in ((0, we_ref), (1, wo_ref)):
            rhs = lanes(x[par], x[par + 2])
            keep = lanes(m[4 * par:4 * par + 4], m[4 * par + 8:4 * par + 12])
            keep = jnp.concatenate([keep, keep], axis=0)[None]
            proj = jnp.dot(w_ref[...], rhs, preferred_element_type=jnp.float32)
            proj = proj.reshape(4, 32, 8, 384)
            acts.append((keep * sigmoid(proj[1]) * proj[0], keep * sigmoid(proj[3]) * proj[2]))
        low = lax.broadcasted_iota(jnp.int32, (32, 8, 384), 1) < 4
        for e, o, ref in ((acts[0][0], acts[1][0], a_ref), (acts[0][1], acts[1][1], b_ref)):
            first = jnp.where(low, e, o)
            second = jnp.where(low, o, e)
            both = jnp.stack([first, second], axis=1).reshape(64, 8, 384).astype(jnp.bfloat16)
            for sec in range(3):
                ref[:, sec, 8 * half:8 * half + 8, :] = both[:, :, 128 * sec:128 * sec + 128]


def project(z, m, gin, w_even, w_odd):
    full = lambda i: (0, 0)
    tile = jax.ShapeDtypeStruct((64, 3, 96, 128), jnp.bfloat16)
    out_spec = pl.BlockSpec((64, 3, 16, 128), lambda i: (0, 0, i, 0))
    return pl.pallas_call(
        project_kernel,
        grid=(6,),
        out_shape=[tile, tile],
        in_specs=[
            pl.BlockSpec((32, 64, 192), lambda i: (i, 0, 0)),
            pl.BlockSpec((32, 192), lambda i: (i, 0)),
            pl.BlockSpec((64, 1), full),
            pl.BlockSpec((1024, 256), full),
            pl.BlockSpec((1024, 256), full),
        ],
        out_specs=[out_spec, out_spec],
        compiler_params=pltpu.CompilerParams(vmem_limit_bytes=48 * 1024 * 1024),
    )(z, m, gin, w_even, w_odd)


def move_kernel(a_ref, b_ref, pa, pb, tr, stage_a, stage_b, sem_a, sem_b, sem_tr, snd, loc):
    bat, z, row = lax.axis_index('batch'), lax.axis_index('col'), lax.axis_index('row')
    y, core = row // 2, row % 2
    size = 64 // CHUNKS

    def flip(v, n, fam):
        return jnp.where(fam == 0, v, n - v)

    def dev(col, r):
        return {'batch': bat, 'col': col, 'row': r}

    def rc(src, dst, send, recv, col, r):
        return pltpu.make_async_remote_copy(
            src_ref=src, dst_ref=dst, send_sem=send, recv_sem=recv, device_id=dev(col, r), device_id_type=MESH)

    def part(ref, c):
        return ref.at[pl.ds(c * size, size)]

    def slot(ref, s, c):
        return ref.at[s, pl.ds(c * size, size)]

    fam = z // 2
    blk = flip(z, 3, fam)
    home = y == fam
    k_src = flip(row, 3, fam)

    def to_home(c):
        return rc(part(a_ref, c), slot(pa, row, c), snd.at[0, c], sem_a.at[row, c], z, z)

    def to_transit(c):
        return rc(part(a_ref, c), slot(tr, blk, c), snd.at[1, c], sem_tr.at[blk, c], flip(k_src, 3, fam), row)

    def b_far(c):
        return rc(part(b_ref, c), slot(pb, row, c), snd.at[2, c], sem_b.at[row, c], z, 2 * (1 - y) + core)

    def b_near(c):
        return rc(part(b_ref, c), slot(pb, row, c), snd.at[3, c], sem_b.at[row, c], z, 2 * y + 1 - core)

    far_row = 2 * (1 - y) + core

    def b_relay(c):
        return rc(slot(pb, far_row, c), slot(pb, far_row, c), snd.at[4, c], sem_b.at[far_row, c], z, 2 * y + 1 - core)

    zz, ii = flip(z, 3, y), flip(row, 3, y)

    def real(kk):
        return flip(jnp.int32(kk), 3, y)

    def right(kk, c):
        k = real(kk)
        return rc(slot(pa, k, c), slot(pa, k, c), snd.at[5 + kk, c], sem_a.at[k, c], jnp.where(y == 0, z + 1, z - 1), row)

    def left(kk, c):
        k = real(kk)
        return rc(slot(pa, k, c), slot(pa, k, c), snd.at[9 + kk, c], sem_a.at[k, c], jnp.where(y == 0, z - 1, z + 1), row)

    ofam = 1 - y
    oz, ok = flip(z, 3, ofam), flip(row, 3, ofam)
    is_way = (oz >= 2) & (ok == oz)

    def up(i2, c):
        return rc(slot(tr, i2, c), slot(pa, row, c), snd.at[13 + i2, c], sem_a.at[row, c], z, flip(jnp.int32(i2), 3, ofam))

    is_src = (ii == zz)
    own_home = home & (row == z)

    cp_a = pltpu.make_async_copy(a_ref, stage_a, loc.at[0])
    cp_b = pltpu.make_async_copy(b_ref, stage_b, loc.at[1])

    @pl.when(own_home)
    def _():
        cp_a.start()

    cp_b.start()

    def for_chunks(f):
        def body(c, _):
            f(c)
            return 0
        lax.fori_loop(0, CHUNKS, body, 0)

    def first_sends(c):
        @pl.when(jnp.logical_not(own_home))
        def _():
            to_home(c).start()

        @pl.when(jnp.logical_not(home))
        def _():
            to_transit(c).start()

    for_chunks(first_sends)

    def b_sends(c):
        b_far(c).start()
        b_near(c).start()

    for_chunks(b_sends)

    @pl.when(own_home)
    def _():
        cp_a.wait()
        out = pltpu.make_async_copy(stage_a, pa.at[row], loc.at[2])
        out.start()
        out.wait()

    cp_b.wait()
    out_b = pltpu.make_async_copy(stage_b, pb.at[row], loc.at[3])
    out_b.start()

    def wait_a(kk, c):
        k = real(kk)

        @pl.when(jnp.logical_not(own_home & (k == row)))
        def _():
            rc(slot(pa, k, c), slot(pa, k, c), snd.at[0, c], sem_a.at[k, c], z, row).wait_recv()

    goes_right = [
        ((zz == 0) & is_src) | ((zz == 1)) | (zz == 2),
        ((zz == 0) & is_src) | ((zz == 1)) | (zz == 2),
        ((zz == 0) & is_src) | (zz == 2),
        ((zz == 0) & is_src),
    ]
    goes_left = [
        (zz == 1) & is_src,
        (zz == 1) & is_src,
        (zz == 1) & is_src,
        ((zz == 1) & is_src) | (zz == 3),
    ]

    def relay(c):
        for kk in range(4):
            wait_a(kk, c)

            @pl.when(goes_right[kk])
            def _():
                right(kk, c).start()

            @pl.when(goes_left[kk])
            def _():
                left(kk, c).start()
            if kk == 1:
                @pl.when(is_way)
                def _():
                    for i2 in range(2):
                        rc(slot(tr, i2, c), slot(tr, i2, c), snd.at[0, c], sem_tr.at[i2, c], z, row).wait_recv()
                        up(i2, c).start()

    for_chunks(relay)

    def b_relays(c):
        rc(slot(pb, far_row, c), slot(pb, far_row, c), snd.at[0, c], sem_b.at[far_row, c], z, row).wait_recv()
        b_relay(c).start()

    for_chunks(b_relays)

    def drain(c):
        for r in (2 * y + 1 - core, 2 * (1 - y) + 1 - core):
            rc(slot(pb, r, c), slot(pb, r, c), snd.at[0, c], sem_b.at[r, c], z, row).wait_recv()

        @pl.when(jnp.logical_not(own_home))
        def _():
            to_home(c).wait_send()

        @pl.when(jnp.logical_not(home))
        def _():
            to_transit(c).wait_send()
        b_far(c).wait_send()
        b_near(c).wait_send()
        b_relay(c).wait_send()
        for kk in range(4):
            @pl.when(goes_right[kk])
            def _():
                right(kk, c).wait_send()

            @pl.when(goes_left[kk])
            def _():
                left(kk, c).wait_send()

        @pl.when(is_way)
        def _():
            for i2 in range(2):
                up(i2, c).wait_send()

    for_chunks(drain)
    out_b.wait()


def move(a, b):
    tile = (64, 3, 96, 128)
    any_spec = pl.BlockSpec(memory_space=pltpu.HBM)
    pa, pb, _ = pl.pallas_call(
        move_kernel,
        out_shape=[jax.ShapeDtypeStruct((n,) + tile, jnp.bfloat16) for n in (4, 4, 2)],
        in_specs=[any_spec] * 2,
        out_specs=[any_spec] * 3,
        scratch_shapes=[
            pltpu.VMEM(tile, jnp.bfloat16),
            pltpu.VMEM(tile, jnp.bfloat16),
            pltpu.SemaphoreType.DMA((4, CHUNKS)),
            pltpu.SemaphoreType.DMA((4, CHUNKS)),
            pltpu.SemaphoreType.DMA((2, CHUNKS)),
            pltpu.SemaphoreType.DMA((15, CHUNKS)),
            pltpu.SemaphoreType.DMA((4,)),
        ],
        compiler_params=pltpu.CompilerParams(has_side_effects=True),
    )(a, b)
    return pa, pb


H_STEP = 4
E_STEPS = 64 // H_STEP
I_STEP = 16


def finish_kernel(pa_ref, pb_ref, z_ref, gin_ref, gout_ref, wg_ref, wo_ref, out_ref, o_ref):
    step = pl.program_id(0)

    @pl.when(step < E_STEPS)
    def _():
        def one(h, _):
            def sides(ref):
                sec = [ref[:, h, s].reshape(384, 128) for s in range(3)]
                return jnp.concatenate([sec[0], sec[2]], axis=1), jnp.concatenate([sec[1], sec[2]], axis=1)

            a_lo, a_hi = sides(pa_ref)
            b_lo, b_hi = sides(pb_ref)
            dims = (((0,), (0,)), ((), ()))
            lo = lax.dot_general(a_lo, b_lo, dims, preferred_element_type=jnp.float32)
            hi = lax.dot_general(a_hi, b_hi, dims, preferred_element_type=jnp.float32)
            hh = step * H_STEP + h
            o_ref[hh, 0:128, 0:128] = lo[0:128, 0:128] + hi[0:128, 0:128]
            o_ref[hh, 128:192, 0:128] = lo[128:192, 0:128] + hi[192:256, 0:128]
            right = jnp.concatenate(
                [lo[0:128, 128:192] + hi[0:128, 192:256], lo[128:192, 128:192] + lo[192:256, 192:256]], axis=0)
            o_ref[hh, :, 128:192] = right
            return 0

        lax.fori_loop(0, H_STEP, one, 0)

    @pl.when(step >= E_STEPS)
    def _():
        base = (step - E_STEPS) * I_STEP
        for q in range(I_STEP // 8):
            rows = pl.ds(pl.multiple_of(base + 8 * q, 8), 8)
            o = o_ref[:, rows, :]
            yv = norm_channels(o, gout_ref[...], 0).astype(jnp.bfloat16).reshape(512, 192)
            upd = jnp.dot(wo_ref[...], yv, preferred_element_type=jnp.float32)
            zv = z_ref[8 * q:8 * q + 8].astype(jnp.float32)
            x = norm_channels(zv, gin_ref[...][None], 1).astype(jnp.bfloat16).reshape(2, 256, 192)
            for s in range(2):
                gate = sigmoid(jnp.dot(wg_ref[...], x[s], preferred_element_type=jnp.float32))
                res = zv[4 * s:4 * s + 4].reshape(256, 192) + gate * upd[256 * s:256 * s + 256]
                out_ref[8 * q + 4 * s:8 * q + 4 * s + 4] = res.astype(jnp.bfloat16).reshape(4, 64, 192)


def finish(pa, pb, z, gin, gout, wg, wo):
    panel = pl.BlockSpec((4, H_STEP, 3, 96, 128), lambda i: (0, jnp.minimum(i, E_STEPS - 1), 0, 0, 0))
    rows = pl.BlockSpec((I_STEP, 64, 192), lambda i: (jnp.maximum(i - E_STEPS, 0), 0, 0))
    full2 = lambda i: (0, 0)
    return pl.pallas_call(
        finish_kernel,
        grid=(E_STEPS + 192 // I_STEP,),
        out_shape=jax.ShapeDtypeStruct((192, 64, 192), jnp.bfloat16),
        in_specs=[
            panel, panel, rows,
            pl.BlockSpec((64, 1), full2),
            pl.BlockSpec((64, 1, 1), lambda i: (0, 0, 0)),
            pl.BlockSpec((256, 256), full2),
            pl.BlockSpec((512, 512), full2),
        ],
        out_specs=rows,
        scratch_shapes=[pltpu.VMEM((64, 192, 192), jnp.float32)],
        compiler_params=pltpu.CompilerParams(vmem_limit_bytes=48 * 1024 * 1024),
    )(pa, pb, z, gin, gout, wg, wo)


def spread(w, n, swap=False):
    t = w.T
    if swap:
        t = t.reshape(32, 2, 64)[:, ::-1].reshape(64, 64)
    eye = jnp.eye(n, dtype=w.dtype)
    return (t[:, None, None, :] * eye[None, :, :, None]).reshape(64 * n, 64 * n)


def solution(mesh):
    tile_spec = P(('batch', 'row'), 'col', None)
    mask_spec = P(('batch', 'row'), 'col')
    replicated = P()

    def local_step(pair, mask, gin, w_l, w_lg, w_r, w_rg, w_g, gout, w_o):
        z = jnp.transpose(pair, (0, 2, 1))
        gin_c = gin.astype(jnp.float32)[:, None]
        gout_c = gout.astype(jnp.float32)[:, None, None]
        w_even = jnp.concatenate([spread(w, 4) for w in (w_l, w_lg, w_r, w_rg)], axis=0)
        w_odd = jnp.concatenate([spread(w, 4, True) for w in (w_l, w_lg, w_r, w_rg)], axis=0)
        eye4, eye8 = jnp.eye(4, dtype=w_g.dtype), jnp.eye(8, dtype=w_o.dtype)
        wg4 = (eye4[:, None, :, None] * w_g.T[None, :, None, :]).reshape(256, 256)
        wo8 = (eye8[:, None, None, :] * w_o.T[None, :, :, None]).reshape(512, 512)
        a, b = project(z, mask, gin_c, w_even, w_odd)
        pa, pb = move(a, b)
        out = finish(pa, pb, z, gin_c, gout_c, wg4, wo8)
        return jnp.transpose(out, (0, 2, 1))

    return jax.shard_map(local_step, mesh=mesh, in_specs=(tile_spec, mask_spec) + (replicated,) * 8, out_specs=tile_spec, check_vma=False)
```

time: 910 us -> 549 us (0.60)
  the two profiles are of different devices: /device:TPU:16 before, /device:TPU:15 now
where the time goes in v1:
time: 549 us; the launch traced here: 548 us
  Pallas kernels  538 us (98%)
  local copies, waits for them, and re-layouts  8.72 us (2%)
    pallas_call x1, Pallas kernels, move(): pl.pallas_call(move_kernel, out_shape=[jax.ShapeDtypeStruct((n,) + tile,...  482 us
    pallas_call x1, Pallas kernels, finish(): pl.pallas_call(finish_kernel, grid=(E_STEPS + 192 // I_STEP,), out_shape=...  42.4 us
    pallas_call x1, Pallas kernels, project(): pl.pallas_call(project_kernel, grid=(6,), out_shape=[tile, tile], in_spec...  13.5 us

profile of v1, /device:TPU:15, one launch (start us, length us, event | category | flops | bytes accessed | tf_op | source)
XLA Modules:
  0.0 548.3 jit_solution(172389988168686623)
XLA Ops:
  0.0 0.8 copy.26
  0.9 0.8 copy.27
  1.8 0.8 copy.24
  2.7 0.8 copy.25
  3.6 0.9 broadcast_multiply_fusion.5
  4.5 0.2 mul.181
  4.8 0.2 mul.184
  5.0 0.2 mul.187
  5.2 0.2 mul.190
  5.4 0.2 mul.194
  5.6 0.2 mul.198
  5.8 0.2 mul.202
  6.1 0.2 mul.206
  6.4 0.1 copy.28.gin_ref
  6.5 13.5 %shard_map.100 = (bf16[64,3,96,128]{3,2,1,0:T(8,128)(2,1)S(1)}, bf16[64,3,96,128]{3,2,1,0:T(8,128)(2,1)}) custom-call(bf16[192,64,192]{2,1,0:T(8,128)(2,1)} %bitcast.30, s32[192,192]{1,0:T(8,128)S(1)} %copy-done.1, f32[64,1]{1,0:T(8,128)S(1)} %copy.28.gin_ref, bf16[1024,256]{1,0:T(8,128)(2,1)S(1)} %get-tuple-element.21.we_ref, ...), custom_call_target="tpu_custom_call" | custom-call | tf_op jit(solution)/shard_map/pallas_call | solution.py:55
  19.9 2.1 copy-done
  22.0 482.2 %shard_map.101 = (bf16[4,64,3,96,128]{4,3,2,1,0:T(8,128)(2,1)}, bf16[4,64,3,96,128]{4,3,2,1,0:T(8,128)(2,1)}, bf16[2,64,3,96,128]{4,3,2,1,0:T(8,128)(2,1)}) custom-call(bf16[64,3,96,128]{3,2,1,0:T(8,128)(2,1)} %copy-done, bf16[64,3,96,128]{3,2,1,0:T(8,128)(2,1)} %get-tuple-element.10.b_ref), custom_call_target="tpu_custom_call" | custom-call | tf_op jit(solution)/shard_map/pallas_call | solution.py:261
  504.3 0.2 broadcast_multiply_fusion.1
  504.5 0.2 mul.210.wg_ref
  504.8 0.1 broadcast_multiply_fusion
  504.9 0.6 mul.214
  505.5 0.2 copy.32.wo_ref
  505.8 0.1 copy.31.gout_ref
  505.9 42.4 %shard_map.102 = bf16[192,64,192]{2,1,0:T(8,128)(2,1)} custom-call(bf16[4,64,3,96,128]{4,3,2,1,0:T(8,128)(2,1)} %get-tuple-element.11.pa_ref, bf16[4,64,3,96,128]{4,3,2,1,0:T(8,128)(2,1)} %get-tuple-element.12.pb_ref, bf16[192,64,192]{2,1,0:T(8,128)(2,1)} %bitcast.31, f32[64,1]{1,0:T(8,128)S(1)} %copy.28.gin_ref, f32[64,1,1]{2,1,0:T(1,128)S(1)} %copy.31.gout_ref, ...), custom_call_target="tpu_custom_call" | custom-call | tf_op jit(solution)/shard_map/pallas_call | solution.py:330
  (21 shorter events, 0.6 us)
Async XLA Ops:
  0.0 6.4 %copy-start.4 = (bf16[64]{0:T(256)(128)(2,1)S(1)}, bf16[64]{0:T(256)(128)(2,1)}, u32[]{:S(2)}) copy-start(bf16[64]{0:T(256)(128)(2,1)} %param.12) | copy-start | bytes 388
  0.0 6.5 %copy-start.1 = (s32[192,192]{1,0:T(8,128)S(1)}, s32[192,192]{1,0:T(8,128)}, u32[]{:S(2)}) copy-start(s32[192,192]{1,0:T(8,128)} %m_ref.1) | copy-start | bytes 442372
  19.9 2.1 copy-start
  22.0 482.2 %copy-start.3 = (bf16[64,64]{1,0:T(8,128)(2,1)S(1)}, bf16[64,64]{1,0:T(8,128)(2,1)}, u32[]{:S(2)}) copy-start(bf16[64,64]{1,0:T(8,128)(2,1)} %param.17) | copy-start | bytes 24580
  22.0 482.7 %copy-start.2 = (bf16[64,64]{1,0:T(8,128)(2,1)S(1)}, bf16[64,64]{1,0:T(8,128)(2,1)}, u32[]{:S(2)}) copy-start(bf16[64,64]{1,0:T(8,128)(2,1)} %param.19) | copy-start | bytes 24580
  22.0 483.7 %copy-start.5 = (bf16[64]{0:T(256)(128)(2,1)S(1)}, bf16[64]{0:T(256)(128)(2,1)}, u32[]{:S(2)}) copy-start(bf16[64]{0:T(256)(128)(2,1)} %param.18) | copy-start | bytes 388

commit v2 on v1

--- a/solution.py
+++ b/solution.py
@@ -7,7 +7,9 @@
 
 LN_EPS = 0.00001
 MESH = pl.DeviceIdType.MESH
-CHUNKS = 8
+CHUNKS = 16
+WAY_LAG = 5
+FAR_LAG = 10
 
 
 def sigmoid(v):
@@ -98,7 +100,7 @@
         return rc(part(a_ref, c), slot(pa, row, c), snd.at[0, c], sem_a.at[row, c], z, z)
 
     def to_transit(c):
-        return rc(part(a_ref, c), slot(tr, blk, c), snd.at[1, c], sem_tr.at[blk, c], flip(k_src, 3, fam), row)
+        return rc(part(a_ref, c), slot(tr, blk, c), snd.at[1, c], sem_tr.at[blk, c], flip(k_src, 3, fam), flip(5 - k_src, 3, fam))
 
     def b_far(c):
         return rc(part(b_ref, c), slot(pb, row, c), snd.at[2, c], sem_b.at[row, c], z, 2 * (1 - y) + core)
@@ -126,10 +128,11 @@
 
     ofam = 1 - y
     oz, ok = flip(z, 3, ofam), flip(row, 3, ofam)
-    is_way = (oz >= 2) & (ok == oz)
+    is_way = (oz >= 2) & (ok == 5 - oz)
+    way_k = flip(oz, 3, ofam)
 
     def up(i2, c):
-        return rc(slot(tr, i2, c), slot(pa, row, c), snd.at[13 + i2, c], sem_a.at[row, c], z, flip(jnp.int32(i2), 3, ofam))
+        return rc(slot(tr, i2, c), slot(pa, way_k, c), snd.at[13 + i2, c], sem_a.at[way_k, c], z, flip(jnp.int32(i2), 3, ofam))
 
     is_src = (ii == zz)
     own_home = home & (row == z)
@@ -159,12 +162,6 @@
             to_transit(c).start()
 
     for_chunks(first_sends)
-
-    def b_sends(c):
-        b_far(c).start()
-        b_near(c).start()
-
-    for_chunks(b_sends)
 
     @pl.when(own_home)
     def _():
@@ -197,35 +194,67 @@
         ((zz == 1) & is_src) | (zz == 3),
     ]
 
-    def relay(c):
-        for kk in range(4):
-            wait_a(kk, c)
-
-            @pl.when(goes_right[kk])
+    def wait_slot(ref, sem, s, c):
+        rc(slot(ref, s, c), slot(ref, s, c), snd.at[0, c], sem.at[s, c], z, row).wait_recv()
+
+    goes = [goes_right[kk] | goes_left[kk] for kk in range(4)]
+    near_lag = [0, 0, 1, 1]
+    forwards = []
+    for kk in range(4):
+        forwards.append((near_lag[kk], kk, goes[kk] & (zz < 2) & is_src))
+    for kk in range(2):
+        forwards.append((1, kk, (zz == 1) & jnp.logical_not(is_src)))
+        forwards.append((2, kk, zz == 2))
+    forwards.append((FAR_LAG, 2, zz == 2))
+    forwards.append((FAR_LAG, 3, zz == 3))
+    forwards.sort(key=lambda f: f[0])
+
+    def in_range(s, lag):
+        return (s >= lag) & (s < CHUNKS + lag)
+
+    def relay(s, _):
+        @pl.when(s < CHUNKS)
+        def _():
+            b_far(s).start()
+            b_near(s).start()
+
+        for lag, kk, who in forwards:
+            @pl.when(in_range(s, lag) & who)
             def _():
-                right(kk, c).start()
-
-            @pl.when(goes_left[kk])
-            def _():
-                left(kk, c).start()
-            if kk == 1:
-                @pl.when(is_way)
+                c = s - lag
+                wait_a(kk, c)
+
+                @pl.when(goes_right[kk])
                 def _():
-                    for i2 in range(2):
-                        rc(slot(tr, i2, c), slot(tr, i2, c), snd.at[0, c], sem_tr.at[i2, c], z, row).wait_recv()
-                        up(i2, c).start()
-
-    for_chunks(relay)
+                    right(kk, c).start()
+
+                @pl.when(goes_left[kk])
+                def _():
+                    left(kk, c).start()
+
+        @pl.when(in_range(s, WAY_LAG) & is_way)
+        def _():
+            c = s - WAY_LAG
+            for i2 in range(2):
+                wait_slot(tr, sem_tr, i2, c)
+                up(i2, c).start()
+        return 0
+
+    lax.fori_loop(0, CHUNKS + FAR_LAG, relay, 0)
 
     def b_relays(c):
-        rc(slot(pb, far_row, c), slot(pb, far_row, c), snd.at[0, c], sem_b.at[far_row, c], z, row).wait_recv()
+        wait_slot(pb, sem_b, far_row, c)
         b_relay(c).start()
 
     for_chunks(b_relays)
 
     def drain(c):
         for r in (2 * y + 1 - core, 2 * (1 - y) + 1 - core):
-            rc(slot(pb, r, c), slot(pb, r, c), snd.at[0, c], sem_b.at[r, c], z, row).wait_recv()
+            wait_slot(pb, sem_b, r, c)
+        for kk in range(4):
+            @pl.when(jnp.logical_not(goes[kk]))
+            def _():
+                wait_a(kk, c)
 
         @pl.when(jnp.logical_not(own_home))
         def _():

time: 549 us -> 409 us (0.74)
  the two profiles are of different devices: /device:TPU:15 before, /device:TPU:16 now
where the time goes in v2:
time: 409 us; the launch traced here: 406 us
  Pallas kernels  395 us (97%)
  local copies, waits for them, and re-layouts  8.72 us (2%)
    pallas_call x1, Pallas kernels, move(): pl.pallas_call(move_kernel, out_shape=[jax.ShapeDtypeStruct((n,) + tile,...  340 us
    pallas_call x1, Pallas kernels, finish(): pl.pallas_call(finish_kernel, grid=(E_STEPS + 192 // I_STEP,), out_shape=...  42.4 us
    pallas_call x1, Pallas kernels, project(): pl.pallas_call(project_kernel, grid=(6,), out_shape=[tile, tile], in_spec...  13.5 us

profile of v2, /device:TPU:16, one launch (start us, length us, event | category | flops | bytes accessed | tf_op | source)
XLA Modules:
  0.0 405.6 jit_solution(548200442078727074)
XLA Ops:
  0.0 0.8 copy.26
  0.9 0.8 copy.27
  1.8 0.8 copy.24
  2.7 0.8 copy.25
  3.6 0.9 broadcast_multiply_fusion.5
  4.5 0.2 mul.181
  4.8 0.2 mul.184
  5.0 0.2 mul.187
  5.2 0.2 mul.190
  5.4 0.2 mul.194
  5.6 0.2 mul.198
  5.8 0.2 mul.202
  6.1 0.2 mul.206
  6.4 0.1 copy.28.gin_ref
  6.5 13.5 %shard_map.100 = (bf16[64,3,96,128]{3,2,1,0:T(8,128)(2,1)S(1)}, bf16[64,3,96,128]{3,2,1,0:T(8,128)(2,1)}) custom-call(bf16[192,64,192]{2,1,0:T(8,128)(2,1)} %bitcast.30, s32[192,192]{1,0:T(8,128)S(1)} %copy-done.1, f32[64,1]{1,0:T(8,128)S(1)} %copy.28.gin_ref, bf16[1024,256]{1,0:T(8,128)(2,1)S(1)} %get-tuple-element.21.we_ref, ...), custom_call_target="tpu_custom_call" | custom-call | tf_op jit(solution)/shard_map/pallas_call | solution.py:57
  19.9 2.1 copy-done
  22.0 339.6 %shard_map.101 = (bf16[4,64,3,96,128]{4,3,2,1,0:T(8,128)(2,1)}, bf16[4,64,3,96,128]{4,3,2,1,0:T(8,128)(2,1)}, bf16[2,64,3,96,128]{4,3,2,1,0:T(8,128)(2,1)}) custom-call(bf16[64,3,96,128]{3,2,1,0:T(8,128)(2,1)} %copy-done, bf16[64,3,96,128]{3,2,1,0:T(8,128)(2,1)} %get-tuple-element.10.b_ref), custom_call_target="tpu_custom_call" | custom-call | tf_op jit(solution)/shard_map/pallas_call | solution.py:290
  361.7 0.2 broadcast_multiply_fusion.1
  361.9 0.2 mul.210.wg_ref
  362.1 0.1 broadcast_multiply_fusion
  362.3 0.6 mul.214
  362.9 0.2 copy.32.wo_ref
  363.1 0.1 copy.31.gout_ref
  363.2 42.4 %shard_map.102 = bf16[192,64,192]{2,1,0:T(8,128)(2,1)} custom-call(bf16[4,64,3,96,128]{4,3,2,1,0:T(8,128)(2,1)} %get-tuple-element.11.pa_ref, bf16[4,64,3,96,128]{4,3,2,1,0:T(8,128)(2,1)} %get-tuple-element.12.pb_ref, bf16[192,64,192]{2,1,0:T(8,128)(2,1)} %bitcast.31, f32[64,1]{1,0:T(8,128)S(1)} %copy.28.gin_ref, f32[64,1,1]{2,1,0:T(1,128)S(1)} %copy.31.gout_ref, ...), custom_call_target="tpu_custom_call" | custom-call | tf_op jit(solution)/shard_map/pallas_call | solution.py:359
  (21 shorter events, 0.6 us)
Async XLA Ops:
  0.0 6.4 %copy-start.4 = (bf16[64]{0:T(256)(128)(2,1)S(1)}, bf16[64]{0:T(256)(128)(2,1)}, u32[]{:S(2)}) copy-start(bf16[64]{0:T(256)(128)(2,1)} %param.12) | copy-start | bytes 388
  0.0 6.5 %copy-start.1 = (s32[192,192]{1,0:T(8,128)S(1)}, s32[192,192]{1,0:T(8,128)}, u32[]{:S(2)}) copy-start(s32[192,192]{1,0:T(8,128)} %m_ref.1) | copy-start | bytes 442372
  19.9 2.1 copy-start
  22.0 339.6 %copy-start.3 = (bf16[64,64]{1,0:T(8,128)(2,1)S(1)}, bf16[64,64]{1,0:T(8,128)(2,1)}, u32[]{:S(2)}) copy-start(bf16[64,64]{1,0:T(8,128)(2,1)} %param.17) | copy-start | bytes 24580
  22.0 340.1 %copy-start.2 = (bf16[64,64]{1,0:T(8,128)(2,1)S(1)}, bf16[64,64]{1,0:T(8,128)(2,1)}, u32[]{:S(2)}) copy-start(bf16[64,64]{1,0:T(8,128)(2,1)} %param.19) | copy-start | bytes 24580
  22.0 341.1 %copy-start.5 = (bf16[64]{0:T(256)(128)(2,1)S(1)}, bf16[64]{0:T(256)(128)(2,1)}, u32[]{:S(2)}) copy-start(bf16[64]{0:T(256)(128)(2,1)} %param.18) | copy-start | bytes 388

commit v3 on v2

--- a/solution.py
+++ b/solution.py
@@ -10,6 +10,8 @@
 CHUNKS = 16
 WAY_LAG = 5
 FAR_LAG = 10
+B_LAG = 9
+SUM_LAG = 13
 
 
 def sigmoid(v):
@@ -66,11 +68,27 @@
             pl.BlockSpec((1024, 256), full),
         ],
         out_specs=[out_spec, out_spec],
-        compiler_params=pltpu.CompilerParams(vmem_limit_bytes=48 * 1024 * 1024),
+        compiler_params=pltpu.CompilerParams(vmem_limit_bytes=60 * 1024 * 1024),
     )(z, m, gin, w_even, w_odd)
 
 
-def move_kernel(a_ref, b_ref, pa, pb, tr, stage_a, stage_b, sem_a, sem_b, sem_tr, snd, loc):
+def channel_sum(pa, pb, h, buf, at):
+    def sides(ref):
+        sec = [ref[:, h, s].reshape(384, 128) for s in range(3)]
+        return jnp.concatenate([sec[0], sec[2]], axis=1), jnp.concatenate([sec[1], sec[2]], axis=1)
+
+    a_lo, a_hi = sides(pa)
+    b_lo, b_hi = sides(pb)
+    dims = (((0,), (0,)), ((), ()))
+    lo = lax.dot_general(a_lo, b_lo, dims, preferred_element_type=jnp.float32)
+    hi = lax.dot_general(a_hi, b_hi, dims, preferred_element_type=jnp.float32)
+    buf[at + (slice(0, 128), slice(0, 128))] = lo[0:128, 0:128] + hi[0:128, 0:128]
+    buf[at + (slice(128, 192), slice(0, 128))] = lo[128:192, 0:128] + hi[192:256, 0:128]
+    buf[at + (slice(None), slice(128, 192))] = jnp.concatenate(
+        [lo[0:128, 128:192] + hi[0:128, 192:256], lo[128:192, 128:192] + lo[192:256, 192:256]], axis=0)
+
+
+def move_kernel(a_ref, b_ref, o_ref, tr, pa, pb, buf, sem_a, sem_b, sem_tr, snd, loc, out_sem):
     bat, z, row = lax.axis_index('batch'), lax.axis_index('col'), lax.axis_index('row')
     y, core = row // 2, row % 2
     size = 64 // CHUNKS
@@ -137,8 +155,8 @@
     is_src = (ii == zz)
     own_home = home & (row == z)
 
-    cp_a = pltpu.make_async_copy(a_ref, stage_a, loc.at[0])
-    cp_b = pltpu.make_async_copy(b_ref, stage_b, loc.at[1])
+    cp_a = pltpu.make_async_copy(a_ref, pa.at[row], loc.at[0])
+    cp_b = pltpu.make_async_copy(b_ref, pb.at[row], loc.at[1])
 
     @pl.when(own_home)
     def _():
@@ -166,13 +184,8 @@
     @pl.when(own_home)
     def _():
         cp_a.wait()
-        out = pltpu.make_async_copy(stage_a, pa.at[row], loc.at[2])
-        out.start()
-        out.wait()
 
     cp_b.wait()
-    out_b = pltpu.make_async_copy(stage_b, pb.at[row], loc.at[3])
-    out_b.start()
 
     def wait_a(kk, c):
         k = real(kk)
@@ -238,24 +251,42 @@
             for i2 in range(2):
                 wait_slot(tr, sem_tr, i2, c)
                 up(i2, c).start()
+        @pl.when(in_range(s, B_LAG))
+        def _():
+            c = s - B_LAG
+            wait_slot(pb, sem_b, far_row, c)
+            b_relay(c).start()
+
+        @pl.when(in_range(s, SUM_LAG))
+        def _():
+            c = s - SUM_LAG
+            for r in (2 * y + 1 - core, 2 * (1 - y) + 1 - core):
+                wait_slot(pb, sem_b, r, c)
+            for kk in range(4):
+                @pl.when(jnp.logical_not(goes[kk]))
+                def _():
+                    wait_a(kk, c)
+
+            @pl.when(c >= 2)
+            def _():
+                sum_out(c - 2).wait()
+
+            def one(h, _):
+                channel_sum(pa, pb, c * size + h, buf, (c % 2, h))
+                return 0
+
+            lax.fori_loop(0, size, one, 0)
+            sum_out(c).start()
         return 0
 
-    lax.fori_loop(0, CHUNKS + FAR_LAG, relay, 0)
-
-    def b_relays(c):
-        wait_slot(pb, sem_b, far_row, c)
-        b_relay(c).start()
-
-    for_chunks(b_relays)
+    def sum_out(c):
+        return pltpu.make_async_copy(buf.at[c % 2], part(o_ref, c), out_sem.at[c % 2])
+
+    lax.fori_loop(0, CHUNKS + SUM_LAG, relay, 0)
+    for c in range(CHUNKS - 2, CHUNKS):
+        sum_out(c).wait()
 
     def drain(c):
-        for r in (2 * y + 1 - core, 2 * (1 - y) + 1 - core):
-            wait_slot(pb, sem_b, r, c)
-        for kk in range(4):
-            @pl.when(jnp.logical_not(goes[kk]))
-            def _():
-                wait_a(kk, c)
-
         @pl.when(jnp.logical_not(own_home))
         def _():
             to_home(c).wait_send()
@@ -281,96 +312,65 @@
                 up(i2, c).wait_send()
 
     for_chunks(drain)
-    out_b.wait()
 
 
 def move(a, b):
     tile = (64, 3, 96, 128)
     any_spec = pl.BlockSpec(memory_space=pltpu.HBM)
-    pa, pb, _ = pl.pallas_call(
+    o, _ = pl.pallas_call(
         move_kernel,
-        out_shape=[jax.ShapeDtypeStruct((n,) + tile, jnp.bfloat16) for n in (4, 4, 2)],
+        out_shape=[jax.ShapeDtypeStruct((64, 192, 192), jnp.float32), jax.ShapeDtypeStruct((2,) + tile, jnp.bfloat16)],
         in_specs=[any_spec] * 2,
-        out_specs=[any_spec] * 3,
+        out_specs=[any_spec] * 2,
         scratch_shapes=[
-            pltpu.VMEM(tile, jnp.bfloat16),
-            pltpu.VMEM(tile, jnp.bfloat16),
+            pltpu.VMEM((4,) + tile, jnp.bfloat16),
+            pltpu.VMEM((4,) + tile, jnp.bfloat16),
+            pltpu.VMEM((2, 64 // CHUNKS, 192, 192), jnp.float32),
             pltpu.SemaphoreType.DMA((4, CHUNKS)),
             pltpu.SemaphoreType.DMA((4, CHUNKS)),
             pltpu.SemaphoreType.DMA((2, CHUNKS)),
             pltpu.SemaphoreType.DMA((15, CHUNKS)),
-            pltpu.SemaphoreType.DMA((4,)),
+            pltpu.SemaphoreType.DMA((2,)),
+            pltpu.SemaphoreType.DMA((2,)),
         ],
-        compiler_params=pltpu.CompilerParams(has_side_effects=True),
+        compiler_params=pltpu.CompilerParams(has_side_effects=True, vmem_limit_bytes=60 * 1024 * 1024),
     )(a, b)
-    return pa, pb
-
-
-H_STEP = 4
-E_STEPS = 64 // H_STEP
+    return o
+
+
 I_STEP = 16
 
 
-def finish_kernel(pa_ref, pb_ref, z_ref, gin_ref, gout_ref, wg_ref, wo_ref, out_ref, o_ref):
-    step = pl.program_id(0)
-
-    @pl.when(step < E_STEPS)
-    def _():
-        def one(h, _):
-            def sides(ref):
-                sec = [ref[:, h, s].reshape(384, 128) for s in range(3)]
-                return jnp.concatenate([sec[0], sec[2]], axis=1), jnp.concatenate([sec[1], sec[2]], axis=1)
-
-            a_lo, a_hi = sides(pa_ref)
-            b_lo, b_hi = sides(pb_ref)
-            dims = (((0,), (0,)), ((), ()))
-            lo = lax.dot_general(a_lo, b_lo, dims, preferred_element_type=jnp.float32)
-            hi = lax.dot_general(a_hi, b_hi, dims, preferred_element_type=jnp.float32)
-            hh = step * H_STEP + h
-            o_ref[hh, 0:128, 0:128] = lo[0:128, 0:128] + hi[0:128, 0:128]
-            o_ref[hh, 128:192, 0:128] = lo[128:192, 0:128] + hi[192:256, 0:128]
-            right = jnp.concatenate(
-                [lo[0:128, 128:192] + hi[0:128, 192:256], lo[128:192, 128:192] + lo[192:256, 192:256]], axis=0)
-            o_ref[hh, :, 128:192] = right
-            return 0
-
-        lax.fori_loop(0, H_STEP, one, 0)
-
-    @pl.when(step >= E_STEPS)
-    def _():
-        base = (step - E_STEPS) * I_STEP
-        for q in range(I_STEP // 8):
-            rows = pl.ds(pl.multiple_of(base + 8 * q, 8), 8)
-            o = o_ref[:, rows, :]
-            yv = norm_channels(o, gout_ref[...], 0).astype(jnp.bfloat16).reshape(512, 192)
-            upd = jnp.dot(wo_ref[...], yv, preferred_element_type=jnp.float32)
-            zv = z_ref[8 * q:8 * q + 8].astype(jnp.float32)
-            x = norm_channels(zv, gin_ref[...][None], 1).astype(jnp.bfloat16).reshape(2, 256, 192)
-            for s in range(2):
-                gate = sigmoid(jnp.dot(wg_ref[...], x[s], preferred_element_type=jnp.float32))
-                res = zv[4 * s:4 * s + 4].reshape(256, 192) + gate * upd[256 * s:256 * s + 256]
-                out_ref[8 * q + 4 * s:8 * q + 4 * s + 4] = res.astype(jnp.bfloat16).reshape(4, 64, 192)
-
-
-def finish(pa, pb, z, gin, gout, wg, wo):
-    panel = pl.BlockSpec((4, H_STEP, 3, 96, 128), lambda i: (0, jnp.minimum(i, E_STEPS - 1), 0, 0, 0))
-    rows = pl.BlockSpec((I_STEP, 64, 192), lambda i: (jnp.maximum(i - E_STEPS, 0), 0, 0))
+def finish_kernel(o_ref, z_ref, gin_ref, gout_ref, wg_ref, wo_ref, out_ref):
+    for q in range(I_STEP // 8):
+        o = o_ref[:, 8 * q:8 * q + 8, :]
+        yv = norm_channels(o, gout_ref[...], 0).astype(jnp.bfloat16).reshape(512, 192)
+        upd = jnp.dot(wo_ref[...], yv, preferred_element_type=jnp.float32)
+        zv = z_ref[8 * q:8 * q + 8].astype(jnp.float32)
+        x = norm_channels(zv, gin_ref[...][None], 1).astype(jnp.bfloat16).reshape(2, 256, 192)
+        for s in range(2):
+            gate = sigmoid(jnp.dot(wg_ref[...], x[s], preferred_element_type=jnp.float32))
+            res = zv[4 * s:4 * s + 4].reshape(256, 192) + gate * upd[256 * s:256 * s + 256]
+            out_ref[8 * q + 4 * s:8 * q + 4 * s + 4] = res.astype(jnp.bfloat16).reshape(4, 64, 192)
+
+
+def finish(o, z, gin, gout, wg, wo):
+    rows = pl.BlockSpec((I_STEP, 64, 192), lambda i: (i, 0, 0))
     full2 = lambda i: (0, 0)
     return pl.pallas_call(
         finish_kernel,
-        grid=(E_STEPS + 192 // I_STEP,),
+        grid=(192 // I_STEP,),
         out_shape=jax.ShapeDtypeStruct((192, 64, 192), jnp.bfloat16),
         in_specs=[
-            panel, panel, rows,
+            pl.BlockSpec((64, I_STEP, 192), lambda i: (0, i, 0)), rows,
             pl.BlockSpec((64, 1), full2),
             pl.BlockSpec((64, 1, 1), lambda i: (0, 0, 0)),
             pl.BlockSpec((256, 256), full2),
             pl.BlockSpec((512, 512), full2),
         ],
         out_specs=rows,
-        scratch_shapes=[pltpu.VMEM((64, 192, 192), jnp.float32)],
-        compiler_params=pltpu.CompilerParams(vmem_limit_bytes=48 * 1024 * 1024),
-    )(pa, pb, z, gin, gout, wg, wo)
+        compiler_params=pltpu.CompilerParams(vmem_limit_bytes=60 * 1024 * 1024),
+    )(o, z, gin, gout, wg, wo)
 
 
 def spread(w, n, swap=False):
@@ -396,8 +396,8 @@
         wg4 = (eye4[:, None, :, None] * w_g.T[None, :, None, :]).reshape(256, 256)
         wo8 = (eye8[:, None, None, :] * w_o.T[None, :, :, None]).reshape(512, 512)
         a, b = project(z, mask, gin_c, w_even, w_odd)
-        pa, pb = move(a, b)
-        out = finish(pa, pb, z, gin_c, gout_c, wg4, wo8)
+        o = move(a, b)
+        out = finish(o, z, gin_c, gout_c, wg4, wo8)
         return jnp.transpose(out, (0, 2, 1))
 
     return jax.shard_map(local_step, mesh=mesh, in_specs=(tile_spec, mask_spec) + (replicated,) * 8, out_specs=tile_spec, check_vma=False)

time: 409 us -> 391 us (0.956)
  Pallas kernels: 395 us -> 373 us
    pallas_call x2, Pallas kernels: 382 us -> 360 us  [the longest x1 341 us: move(): pl.pallas_call(move_kernel, out_shape=[jax.ShapeDtypeStruct((64, 192, 192...]
where the time goes in v3:
time: 391 us; the launch traced here: 385 us
  Pallas kernels  373 us (95%)
  local copies, waits for them, and re-layouts  9.3 us (2%)
    pallas_call x1, Pallas kernels, move(): pl.pallas_call(move_kernel, out_shape=[jax.ShapeDtypeStruct((64, 192, 192...  341 us
    pallas_call x1, Pallas kernels, finish(): pl.pallas_call(finish_kernel, grid=(192 // I_STEP,), out_shape=jax.ShapeD...  18.2 us
    pallas_call x1, Pallas kernels, project(): pl.pallas_call(project_kernel, grid=(6,), out_shape=[tile, tile], in_spec...  13.9 us

profile of v3, /device:TPU:16, one launch (start us, length us, event | category | flops | bytes accessed | tf_op | source)
XLA Modules:
  0.0 385.1 jit_solution(12298325309940624162)
XLA Ops:
  0.0 0.8 copy.26
  0.9 0.8 copy.27
  1.8 0.8 copy.24
  2.7 0.8 copy.25
  3.6 0.9 broadcast_multiply_fusion.5
  4.5 0.2 mul.181
  4.7 0.2 mul.184
  4.9 0.2 mul.187
  5.2 0.2 mul.190
  5.4 0.2 mul.194
  5.6 0.2 mul.198
  5.8 0.2 mul.202
  6.0 0.2 mul.206
  6.2 1.0 pad_maximum_fusion
  7.3 0.7 copy.28.gin_ref
  8.0 13.9 %shard_map.100 = (bf16[64,3,96,128]{3,2,1,0:T(8,128)(2,1)}, bf16[64,3,96,128]{3,2,1,0:T(8,128)(2,1)}) custom-call(bf16[192,64,192]{2,1,0:T(8,128)(2,1)} %bitcast.30, s32[192,192]{1,0:T(8,128)} %m_ref.1, f32[64,1]{1,0:T(8,128)} %copy.28.gin_ref, bf16[1024,256]{1,0:T(8,128)(2,1)} %get-tuple-element.19.we_ref, bf16[1024,256]{1,0:T(8,128)(2,1)} %get-tuple-element.20.wo_ref), custom_call_target="tpu_custom_call" | custom-call | tf_op jit(solution)/shard_map/pallas_call | solution.py:59
  21.9 341.4 %shard_map.101 = (f32[64,192,192]{2,1,0:T(8,128)}, bf16[2,64,3,96,128]{4,3,2,1,0:T(8,128)(2,1)}) custom-call(bf16[64,3,96,128]{3,2,1,0:T(8,128)(2,1)} %get-tuple-element.8.a_ref, bf16[64,3,96,128]{3,2,1,0:T(8,128)(2,1)} %get-tuple-element.9.b_ref), custom_call_target="tpu_custom_call" | custom-call | tf_op jit(solution)/shard_map/pallas_call | solution.py:320
  363.4 0.2 broadcast_multiply_fusion.1
  363.5 0.9 mul.210.wg_ref
  364.4 0.1 broadcast_multiply_fusion
  364.6 0.6 mul.214
  365.2 1.0 copy.32.wo_ref
  366.2 0.7 copy.31.gout_ref
  366.9 18.2 %shard_map.102 = bf16[192,64,192]{2,1,0:T(8,128)(2,1)} custom-call(f32[64,192,192]{2,1,0:T(8,128)} %get-tuple-element.10.o_ref, bf16[192,64,192]{2,1,0:T(8,128)(2,1)} %bitcast.31, f32[64,1]{1,0:T(8,128)} %copy.28.gin_ref, f32[64,1,1]{2,1,0:T(1,128)} %copy.31.gout_ref, bf16[256,256]{1,0:T(8,128)(2,1)} %mul.210.wg_ref, bf16[512,512]{1,0:T(8,128)(2,1)} %copy.32.wo_ref), custom_call_target="tpu_custom_call" | custom-call | tf_op jit(solution)/shard_map/pallas_call | solution.py:360
  (17 shorter events, 0.5 us)
Async XLA Ops:
  0.0 7.3 %copy-start.2 = (bf16[64]{0:T(256)(128)(2,1)S(1)}, bf16[64]{0:T(256)(128)(2,1)}, u32[]{:S(2)}) copy-start(bf16[64]{0:T(256)(128)(2,1)} %param.12) | copy-start | bytes 388
  21.8 341.4 %copy-start.1 = (bf16[64,64]{1,0:T(8,128)(2,1)S(1)}, bf16[64,64]{1,0:T(8,128)(2,1)}, u32[]{:S(2)}) copy-start(bf16[64,64]{1,0:T(8,128)(2,1)} %param.17) | copy-start | bytes 24580
  21.8 342.6 %copy-start = (bf16[64,64]{1,0:T(8,128)(2,1)S(1)}, bf16[64,64]{1,0:T(8,128)(2,1)}, u32[]{:S(2)}) copy-start(bf16[64,64]{1,0:T(8,128)(2,1)} %param.19) | copy-start | bytes 24580
  21.9 344.4 %copy-start.3 = (bf16[64]{0:T(256)(128)(2,1)S(1)}, bf16[64]{0:T(256)(128)(2,1)}, u32[]{:S(2)}) copy-start(bf16[64]{0:T(256)(128)(2,1)} %param.18) | copy-start | bytes 388

commit v4 on v3

--- a/solution.py
+++ b/solution.py
@@ -7,11 +7,16 @@
 
 LN_EPS = 0.00001
 MESH = pl.DeviceIdType.MESH
-CHUNKS = 16
-WAY_LAG = 5
-FAR_LAG = 10
-B_LAG = 9
-SUM_LAG = 13
+CHUNKS = 32
+NEAR_LAG = 1
+CROSS_LAG = 2
+HOP_LAG = 3
+PASS_LAG = 5
+WAY_LAG = 3
+B_LAG = 3
+EDGE_LAG = 3
+SHARE_LAG = 6
+SUM_LAG = 9
 
 
 def sigmoid(v):
@@ -82,13 +87,15 @@
     dims = (((0,), (0,)), ((), ()))
     lo = lax.dot_general(a_lo, b_lo, dims, preferred_element_type=jnp.float32)
     hi = lax.dot_general(a_hi, b_hi, dims, preferred_element_type=jnp.float32)
-    buf[at + (slice(0, 128), slice(0, 128))] = lo[0:128, 0:128] + hi[0:128, 0:128]
-    buf[at + (slice(128, 192), slice(0, 128))] = lo[128:192, 0:128] + hi[192:256, 0:128]
-    buf[at + (slice(None), slice(128, 192))] = jnp.concatenate(
+    wide = jnp.concatenate([lo[0:128, 0:128] + hi[0:128, 0:128], lo[128:192, 0:128] + hi[192:256, 0:128]], axis=0)
+    rest = jnp.concatenate(
         [lo[0:128, 128:192] + hi[0:128, 192:256], lo[128:192, 128:192] + lo[192:256, 192:256]], axis=0)
-
-
-def move_kernel(a_ref, b_ref, o_ref, tr, pa, pb, buf, sem_a, sem_b, sem_tr, snd, loc, out_sem):
+    buf[at + (0,)] = wide[0:96]
+    buf[at + (1,)] = wide[96:192]
+    buf[at + (2,)] = jnp.concatenate([rest[0:96], rest[96:192]], axis=1)
+
+
+def move_kernel(a_ref, b_ref, o_ref, tr, pa, pb, pe, buf, sem_a, sem_b, sem_e, sem_tr, sem_o, snd, loc, out_sem):
     bat, z, row = lax.axis_index('batch'), lax.axis_index('col'), lax.axis_index('row')
     y, core = row // 2, row % 2
     size = 64 // CHUNKS
@@ -108,61 +115,86 @@
 
     def slot(ref, s, c):
         return ref.at[s, pl.ds(c * size, size)]
+
+    def wait_slot(ref, sem, s, c):
+        rc(slot(ref, s, c), slot(ref, s, c), snd.at[0, c], sem.at[s, c], z, row).wait_recv()
+
+    partner, across = 2 * y + 1 - core, 2 * (1 - y) + core
+    diagonal = 2 * (1 - y) + 1 - core
 
     fam = z // 2
     blk = flip(z, 3, fam)
     home = y == fam
     k_src = flip(row, 3, fam)
+    own_home = home & (row == z)
+    sends_far = jnp.logical_not(home) & ((k_src == 3) | (blk == 1))
 
     def to_home(c):
         return rc(part(a_ref, c), slot(pa, row, c), snd.at[0, c], sem_a.at[row, c], z, z)
 
-    def to_transit(c):
-        return rc(part(a_ref, c), slot(tr, blk, c), snd.at[1, c], sem_tr.at[blk, c], flip(k_src, 3, fam), flip(5 - k_src, 3, fam))
-
-    def b_far(c):
-        return rc(part(b_ref, c), slot(pb, row, c), snd.at[2, c], sem_b.at[row, c], z, 2 * (1 - y) + core)
-
-    def b_near(c):
-        return rc(part(b_ref, c), slot(pb, row, c), snd.at[3, c], sem_b.at[row, c], z, 2 * y + 1 - core)
-
-    far_row = 2 * (1 - y) + core
-
-    def b_relay(c):
-        return rc(slot(pb, far_row, c), slot(pb, far_row, c), snd.at[4, c], sem_b.at[far_row, c], z, 2 * y + 1 - core)
+    def to_way(c):
+        return rc(part(a_ref, c), slot(tr, blk, c), snd.at[1, c], sem_tr.at[blk, c], flip(jnp.int32(2), 3, fam), row)
 
     zz, ii = flip(z, 3, y), flip(row, 3, y)
+    is_src = ii == zz
+    inner = jnp.where(y == 0, z - 1, z + 1)
+    outer = jnp.where(y == 0, z + 1, z - 1)
 
     def real(kk):
         return flip(jnp.int32(kk), 3, y)
 
+    def hop(kk, c, n, col):
+        k = real(kk)
+        return rc(slot(pa, k, c), slot(pa, k, c), snd.at[n + kk, c], sem_a.at[k, c], col, row)
+
     def right(kk, c):
-        k = real(kk)
-        return rc(slot(pa, k, c), slot(pa, k, c), snd.at[5 + kk, c], sem_a.at[k, c], jnp.where(y == 0, z + 1, z - 1), row)
+        return hop(kk, c, 2, outer)
 
     def left(kk, c):
-        k = real(kk)
-        return rc(slot(pa, k, c), slot(pa, k, c), snd.at[9 + kk, c], sem_a.at[k, c], jnp.where(y == 0, z - 1, z + 1), row)
+        return hop(kk, c, 6, inner)
+
+    goes_right = [
+        (zz == 1) | ((zz == 0) & is_src),
+        (zz == 1) | ((zz == 0) & is_src),
+        ((zz == 1) & (ii == 0)) | ((zz == 0) & is_src),
+        (zz == 0) & is_src,
+    ]
+    goes_left = [(zz == 1) & is_src] * 4
+    goes = [goes_right[kk] | goes_left[kk] for kk in range(4)]
 
     ofam = 1 - y
     oz, ok = flip(z, 3, ofam), flip(row, 3, ofam)
-    is_way = (oz >= 2) & (ok == 5 - oz)
-    way_k = flip(oz, 3, ofam)
+    ways = [(oz == 2) & (ok == 3), oz == 2]
 
     def up(i2, c):
-        return rc(slot(tr, i2, c), slot(pa, way_k, c), snd.at[13 + i2, c], sem_a.at[way_k, c], z, flip(jnp.int32(i2), 3, ofam))
-
-    is_src = (ii == zz)
-    own_home = home & (row == z)
-
-    cp_a = pltpu.make_async_copy(a_ref, pa.at[row], loc.at[0])
-    cp_b = pltpu.make_async_copy(b_ref, pb.at[row], loc.at[1])
-
-    @pl.when(own_home)
-    def _():
-        cp_a.start()
-
-    cp_b.start()
+        return rc(slot(tr, i2, c), slot(pa, row, c), snd.at[10 + i2, c], sem_a.at[row, c], z, flip(jnp.int32(i2), 3, ofam))
+
+    is_edge, is_inner = zz == 3, zz == 2
+    not_edge = jnp.logical_not(is_edge)
+
+    def b_far(c):
+        return rc(part(b_ref, c), slot(pb, row, c), snd.at[12, c], sem_b.at[row, c], z, across)
+
+    def b_near(c):
+        return rc(part(b_ref, c), slot(pb, row, c), snd.at[13, c], sem_b.at[row, c], z, partner)
+
+    def b_relay(c):
+        return rc(slot(pb, across, c), slot(pb, across, c), snd.at[14, c], sem_b.at[across, c], z, partner)
+
+    def e_own(c):
+        return rc(part(b_ref, c), slot(pe, row, c), snd.at[13, c], sem_e.at[row, c], inner, row)
+
+    def e_far(c):
+        return rc(slot(pb, across, c), slot(pe, across, c), snd.at[14, c], sem_e.at[across, c], inner, row)
+
+    def e_share(r, n, c):
+        return rc(slot(pe, r, c), slot(pe, r, c), snd.at[n, c], sem_e.at[r, c], z, partner)
+
+    def o_edge(c):
+        return rc(buf.at[2 + c % 2], part(o_ref, c), snd.at[17, c], sem_o.at[c], outer, row)
+
+    def o_own(c):
+        return pltpu.make_async_copy(buf.at[c % 2], part(o_ref, c), out_sem.at[c % 2])
 
     def for_chunks(f):
         def body(c, _):
@@ -170,16 +202,14 @@
             return 0
         lax.fori_loop(0, CHUNKS, body, 0)
 
-    def first_sends(c):
-        @pl.when(jnp.logical_not(own_home))
-        def _():
-            to_home(c).start()
-
-        @pl.when(jnp.logical_not(home))
-        def _():
-            to_transit(c).start()
-
-    for_chunks(first_sends)
+    cp_a = pltpu.make_async_copy(a_ref, pa.at[row], loc.at[0])
+    cp_b = pltpu.make_async_copy(b_ref, pb.at[row], loc.at[1])
+
+    @pl.when(own_home)
+    def _():
+        cp_a.start()
+
+    cp_b.start()
 
     @pl.when(own_home)
     def _():
@@ -192,44 +222,36 @@
 
         @pl.when(jnp.logical_not(own_home & (k == row)))
         def _():
-            rc(slot(pa, k, c), slot(pa, k, c), snd.at[0, c], sem_a.at[k, c], z, row).wait_recv()
-
-    goes_right = [
-        ((zz == 0) & is_src) | ((zz == 1)) | (zz == 2),
-        ((zz == 0) & is_src) | ((zz == 1)) | (zz == 2),
-        ((zz == 0) & is_src) | (zz == 2),
-        ((zz == 0) & is_src),
-    ]
-    goes_left = [
-        (zz == 1) & is_src,
-        (zz == 1) & is_src,
-        (zz == 1) & is_src,
-        ((zz == 1) & is_src) | (zz == 3),
-    ]
-
-    def wait_slot(ref, sem, s, c):
-        rc(slot(ref, s, c), slot(ref, s, c), snd.at[0, c], sem.at[s, c], z, row).wait_recv()
-
-    goes = [goes_right[kk] | goes_left[kk] for kk in range(4)]
-    near_lag = [0, 0, 1, 1]
-    forwards = []
-    for kk in range(4):
-        forwards.append((near_lag[kk], kk, goes[kk] & (zz < 2) & is_src))
-    for kk in range(2):
-        forwards.append((1, kk, (zz == 1) & jnp.logical_not(is_src)))
-        forwards.append((2, kk, zz == 2))
-    forwards.append((FAR_LAG, 2, zz == 2))
-    forwards.append((FAR_LAG, 3, zz == 3))
-    forwards.sort(key=lambda f: f[0])
+            wait_slot(pa, sem_a, k, c)
+
+    forwards = [(NEAR_LAG, 0, (zz < 2) & is_src), (NEAR_LAG, 1, (zz < 2) & is_src)]
+    forwards += [(CROSS_LAG, kk, (zz < 2) & is_src) for kk in (2, 3)]
+    forwards += [(HOP_LAG, kk, (zz == 1) & (ii == 0)) for kk in (0, 1)]
+    forwards += [(PASS_LAG, 2, (zz == 1) & (ii == 0))]
 
     def in_range(s, lag):
         return (s >= lag) & (s < CHUNKS + lag)
 
-    def relay(s, _):
+    def step(s, _):
         @pl.when(s < CHUNKS)
         def _():
+            @pl.when(jnp.logical_not(own_home))
+            def _():
+                to_home(s).start()
+
+            @pl.when(sends_far)
+            def _():
+                to_way(s).start()
+
             b_far(s).start()
-            b_near(s).start()
+
+            @pl.when(is_edge)
+            def _():
+                e_own(s).start()
+
+            @pl.when(not_edge)
+            def _():
+                b_near(s).start()
 
         for lag, kk, who in forwards:
             @pl.when(in_range(s, lag) & who)
@@ -245,58 +267,111 @@
                 def _():
                     left(kk, c).start()
 
-        @pl.when(in_range(s, WAY_LAG) & is_way)
+        @pl.when(in_range(s, WAY_LAG))
         def _():
             c = s - WAY_LAG
             for i2 in range(2):
-                wait_slot(tr, sem_tr, i2, c)
-                up(i2, c).start()
-        @pl.when(in_range(s, B_LAG))
+                @pl.when(ways[i2])
+                def _():
+                    wait_slot(tr, sem_tr, i2, c)
+                    up(i2, c).start()
+
+        @pl.when(in_range(s, EDGE_LAG) & is_edge)
+        def _():
+            c = s - EDGE_LAG
+            wait_slot(pb, sem_b, across, c)
+            e_far(c).start()
+
+        @pl.when(in_range(s, B_LAG) & not_edge)
         def _():
             c = s - B_LAG
-            wait_slot(pb, sem_b, far_row, c)
+            wait_slot(pb, sem_b, across, c)
             b_relay(c).start()
 
-        @pl.when(in_range(s, SUM_LAG))
+        for lag, r, n in ((EDGE_LAG, row, 15), (SHARE_LAG, across, 16)):
+            @pl.when(in_range(s, lag) & is_inner)
+            def _():
+                c = s - lag
+                wait_slot(pe, sem_e, r, c)
+                e_share(r, n, c).start()
+
+        @pl.when(in_range(s, SUM_LAG) & not_edge)
         def _():
             c = s - SUM_LAG
-            for r in (2 * y + 1 - core, 2 * (1 - y) + 1 - core):
+            for r in (partner, diagonal):
                 wait_slot(pb, sem_b, r, c)
             for kk in range(4):
                 @pl.when(jnp.logical_not(goes[kk]))
                 def _():
                     wait_a(kk, c)
 
+            @pl.when(is_inner)
+            def _():
+                for r in (partner, diagonal):
+                    wait_slot(pe, sem_e, r, c)
+
+                @pl.when(c >= 2)
+                def _():
+                    o_edge(c - 2).wait_send()
+
+                def edge(h, _):
+                    channel_sum(pa, pe, c * size + h, buf, (2 + c % 2, h))
+                    return 0
+
+                lax.fori_loop(0, size, edge, 0)
+                o_edge(c).start()
+
             @pl.when(c >= 2)
             def _():
-                sum_out(c - 2).wait()
-
-            def one(h, _):
+                o_own(c - 2).wait()
+
+            def own(h, _):
                 channel_sum(pa, pb, c * size + h, buf, (c % 2, h))
                 return 0
 
-            lax.fori_loop(0, size, one, 0)
-            sum_out(c).start()
+            lax.fori_loop(0, size, own, 0)
+            o_own(c).start()
         return 0
 
-    def sum_out(c):
-        return pltpu.make_async_copy(buf.at[c % 2], part(o_ref, c), out_sem.at[c % 2])
-
-    lax.fori_loop(0, CHUNKS + SUM_LAG, relay, 0)
-    for c in range(CHUNKS - 2, CHUNKS):
-        sum_out(c).wait()
+    lax.fori_loop(0, CHUNKS + SUM_LAG, step, 0)
+
+    @pl.when(not_edge)
+    def _():
+        for c in range(CHUNKS - 2, CHUNKS):
+            o_own(c).wait()
+
+    @pl.when(is_inner)
+    def _():
+        for c in range(CHUNKS - 2, CHUNKS):
+            o_edge(c).wait_send()
 
     def drain(c):
         @pl.when(jnp.logical_not(own_home))
         def _():
             to_home(c).wait_send()
 
-        @pl.when(jnp.logical_not(home))
-        def _():
-            to_transit(c).wait_send()
+        @pl.when(sends_far)
+        def _():
+            to_way(c).wait_send()
+
         b_far(c).wait_send()
-        b_near(c).wait_send()
-        b_relay(c).wait_send()
+
+        @pl.when(not_edge)
+        def _():
+            b_near(c).wait_send()
+            b_relay(c).wait_send()
+
+        @pl.when(is_edge)
+        def _():
+            e_own(c).wait_send()
+            e_far(c).wait_send()
+            rc(buf.at[0], part(o_ref, c), snd.at[0, c], sem_o.at[c], z, row).wait_recv()
+
+        @pl.when(is_inner)
+        def _():
+            e_share(row, 15, c).wait_send()
+            e_share(across, 16, c).wait_send()
+
         for kk in range(4):
             @pl.when(goes_right[kk])
             def _():
@@ -306,9 +381,9 @@
             def _():
                 left(kk, c).wait_send()
 
-        @pl.when(is_way)
-        def _():
-            for i2 in range(2):
+        for i2 in range(2):
+            @pl.when(ways[i2])
+            def _():
                 up(i2, c).wait_send()
 
     for_chunks(drain)
@@ -319,21 +394,21 @@
     any_spec = pl.BlockSpec(memory_space=pltpu.HBM)
     o, _ = pl.pallas_call(
         move_kernel,
-        out_shape=[jax.ShapeDtypeStruct((64, 192, 192), jnp.float32), jax.ShapeDtypeStruct((2,) + tile, jnp.bfloat16)],
+        out_shape=[jax.ShapeDtypeStruct(tile, jnp.float32), jax.ShapeDtypeStruct((2,) + tile, jnp.bfloat16)],
         in_specs=[any_spec] * 2,
         out_specs=[any_spec] * 2,
-        scratch_shapes=[
-            pltpu.VMEM((4,) + tile, jnp.bfloat16),
-            pltpu.VMEM((4,) + tile, jnp.bfloat16),
-            pltpu.VMEM((2, 64 // CHUNKS, 192, 192), jnp.float32),
+        scratch_shapes=[pltpu.VMEM((4,) + tile, jnp.bfloat16)] * 3 + [
+            pltpu.VMEM((4, 64 // CHUNKS, 3, 96, 128), jnp.float32),
+            pltpu.SemaphoreType.DMA((4, CHUNKS)),
             pltpu.SemaphoreType.DMA((4, CHUNKS)),
             pltpu.SemaphoreType.DMA((4, CHUNKS)),
             pltpu.SemaphoreType.DMA((2, CHUNKS)),
-            pltpu.SemaphoreType.DMA((15, CHUNKS)),
+            pltpu.SemaphoreType.DMA((CHUNKS,)),
+            pltpu.SemaphoreType.DMA((18, CHUNKS)),
             pltpu.SemaphoreType.DMA((2,)),
             pltpu.SemaphoreType.DMA((2,)),
         ],
-        compiler_params=pltpu.CompilerParams(has_side_effects=True, vmem_limit_bytes=60 * 1024 * 1024),
+        compiler_params=pltpu.CompilerParams(has_side_effects=True, vmem_limit_bytes=67043328),
     )(a, b)
     return o
 
@@ -341,9 +416,12 @@
 I_STEP = 16
 
 
-def finish_kernel(o_ref, z_ref, gin_ref, gout_ref, wg_ref, wo_ref, out_ref):
+def finish_kernel(wide_ref, rest_ref, z_ref, gin_ref, gout_ref, wg_ref, wo_ref, out_ref):
+    upper = pl.program_id(0) >= 96 // I_STEP
     for q in range(I_STEP // 8):
-        o = o_ref[:, 8 * q:8 * q + 8, :]
+        rest = rest_ref[:, 0, 8 * q:8 * q + 8, :]
+        rest = jnp.where(upper, rest[:, :, 64:], rest[:, :, :64])
+        o = jnp.concatenate([wide_ref[:, 0, 8 * q:8 * q + 8, :], rest], axis=2)
         yv = norm_channels(o, gout_ref[...], 0).astype(jnp.bfloat16).reshape(512, 192)
         upd = jnp.dot(wo_ref[...], yv, preferred_element_type=jnp.float32)
         zv = z_ref[8 * q:8 * q + 8].astype(jnp.float32)
@@ -357,12 +435,15 @@
 def finish(o, z, gin, gout, wg, wo):
     rows = pl.BlockSpec((I_STEP, 64, 192), lambda i: (i, 0, 0))
     full2 = lambda i: (0, 0)
+    half = 96 // I_STEP
     return pl.pallas_call(
         finish_kernel,
         grid=(192 // I_STEP,),
         out_shape=jax.ShapeDtypeStruct((192, 64, 192), jnp.bfloat16),
         in_specs=[
-            pl.BlockSpec((64, I_STEP, 192), lambda i: (0, i, 0)), rows,
+            pl.BlockSpec((64, 1, I_STEP, 128), lambda i: (0, i // half, i % half, 0)),
+            pl.BlockSpec((64, 1, I_STEP, 128), lambda i: (0, 2, i % half, 0)),
+            rows,
             pl.BlockSpec((64, 1), full2),
             pl.BlockSpec((64, 1, 1), lambda i: (0, 0, 0)),
             pl.BlockSpec((256, 256), full2),
@@ -370,7 +451,7 @@
         ],
         out_specs=rows,
         compiler_params=pltpu.CompilerParams(vmem_limit_bytes=60 * 1024 * 1024),
-    )(o, z, gin, gout, wg, wo)
+    )(o, o, z, gin, gout, wg, wo)
 
 
 def spread(w, n, swap=False):

time: 391 us -> 370 us (0.946); the launches traced: 385 us -> 369 us
  Pallas kernels: 373 us -> 354 us
    pallas_call x1, Pallas kernels: 341 us -> 321 us  [move(): pl.pallas_call(move_kernel, out_shape=[jax.ShapeDtypeStruct(tile, jnp.flo...]
where the time goes in v4:
time: 370 us; the launch traced here: 369 us
  Pallas kernels  354 us (96%)
  local copies, waits for them, and re-layouts  9.96 us (3%)
  other arithmetic  4.3 us (1%)
    pallas_call x1, Pallas kernels, move(): pl.pallas_call(move_kernel, out_shape=[jax.ShapeDtypeStruct(tile, jnp.flo...  321 us
    pallas_call x1, Pallas kernels, finish(): pl.pallas_call(finish_kernel, grid=(192 // I_STEP,), out_shape=jax.ShapeD...  19.3 us
    pallas_call x1, Pallas kernels, project(): pl.pallas_call(project_kernel, grid=(6,), out_shape=[tile, tile], in_spec...  13.9 us

profile of v4, /device:TPU:16, one launch (start us, length us, event | category | flops | bytes accessed | tf_op | source)
XLA Modules:
  0.0 368.8 jit_solution(56244427638916710)
XLA Ops:
  0.0 0.8 copy.26
  0.9 0.8 copy.27
  1.8 0.8 copy.24
  2.7 0.8 copy.25
  3.6 0.9 broadcast_multiply_fusion.5
  4.5 0.2 mul.181
  4.8 0.2 mul.184
  5.2 0.2 mul.190
  5.4 0.2 mul.194
  5.6 0.2 mul.198
  5.8 0.2 mul.202
  6.3 1.0 pad_maximum_fusion
  7.3 0.7 copy.28.gin_ref
  8.0 13.9 %shard_map.100 = (bf16[64,3,96,128]{3,2,1,0:T(8,128)(2,1)}, bf16[64,3,96,128]{3,2,1,0:T(8,128)(2,1)}) custom-call(bf16[192,64,192]{2,1,0:T(8,128)(2,1)} %bitcast.30, s32[192,192]{1,0:T(8,128)} %m_ref.1, f32[64,1]{1,0:T(8,128)} %copy.28.gin_ref, bf16[1024,256]{1,0:T(8,128)(2,1)} %get-tuple-element.19.we_ref, bf16[1024,256]{1,0:T(8,128)(2,1)} %get-tuple-element.20.wo_ref), custom_call_target="tpu_custom_call" | custom-call | tf_op jit(solution)/shard_map/pallas_call | solution.py:64
  21.9 321.2 %shard_map.101 = (f32[64,3,96,128]{3,2,1,0:T(8,128)}, bf16[2,64,3,96,128]{4,3,2,1,0:T(8,128)(2,1)}) custom-call(bf16[64,3,96,128]{3,2,1,0:T(8,128)(2,1)} %get-tuple-element.8.a_ref, bf16[64,3,96,128]{3,2,1,0:T(8,128)(2,1)} %get-tuple-element.9.b_ref), custom_call_target="tpu_custom_call" | custom-call | tf_op jit(solution)/shard_map/pallas_call | solution.py:395
  343.2 0.8 copy.29
  344.0 0.8 broadcast_multiply_fusion.1
  344.8 0.9 mul.210.wg_ref
  345.7 0.9 broadcast_multiply_fusion
  346.6 0.6 mul.214
  347.2 1.0 copy.32.wo_ref
  348.2 0.7 bitcast_convert_fusion
  348.8 0.7 copy.31.gout_ref
  349.5 19.3 %shard_map.102 = bf16[192,64,192]{2,1,0:T(8,128)(2,1)} custom-call(f32[64,3,96,128]{3,2,1,0:T(8,128)} %get-tuple-element.10.wide_ref.rest_ref, f32[64,3,96,128]{3,2,1,0:T(8,128)} %get-tuple-element.10.wide_ref.rest_ref, bf16[192,64,192]{2,1,0:T(8,128)(2,1)} %bitcast.31, f32[64,1]{1,0:T(8,128)} %copy.28.gin_ref, f32[64,1,1]{2,1,0:T(1,128)} %copy.31.gout_ref, ...), custom_call_target="tpu_custom_call" | custom-call | tf_op jit(solution)/shard_map/pallas_call | solution.py:439
  (13 shorter events, 0.8 us)
Async XLA Ops:
  0.0 7.3 %copy-start.1 = (bf16[64]{0:T(256)(128)(2,1)S(1)}, bf16[64]{0:T(256)(128)(2,1)}, u32[]{:S(2)}) copy-start(bf16[64]{0:T(256)(128)(2,1)} %param.12) | copy-start | bytes 388
  3.6 0.9 copy-start

commit v5 on v4

--- a/solution.py
+++ b/solution.py
@@ -15,8 +15,8 @@
 WAY_LAG = 3
 B_LAG = 3
 EDGE_LAG = 3
-SHARE_LAG = 6
 SUM_LAG = 9
+INNER_LAG = 7
 
 
 def sigmoid(v):
@@ -30,25 +30,47 @@
     return cen * lax.rsqrt(var + LN_EPS) * gain
 
 
-def project_kernel(z_ref, m_ref, gin_ref, we_ref, wo_ref, a_ref, b_ref):
-    gain = gin_ref[...][None]
+def lanes(p, q):
+    return jnp.concatenate([p[..., :128], q[..., :128], p[..., 128:], q[..., 128:]], axis=-1)
+
+
+def ids(shape, axis):
+    return lax.broadcasted_iota(jnp.int32, shape, axis)
+
+
+def pick(sel, w):
+    return lax.dot_general(sel.astype(jnp.bfloat16), w, (((1,), (1,)), ((), ())), preferred_element_type=jnp.float32)
+
+
+def column(sel, row):
+    return jnp.sum(jnp.where(sel, row.astype(jnp.float32), 0.0), axis=1, keepdims=True)
+
+
+def project_kernel(z_ref, m_ref, gin_ref, wl_ref, wlg_ref, wr_ref, wrg_ref, a_ref, b_ref, gain_ref, we_ref, wo_ref):
+    @pl.when(pl.program_id(0) == 0)
+    def _():
+        gain_ref[...] = jnp.broadcast_to(column(ids((64, 64), 0) == ids((64, 64), 1), gin_ref[...]), (64, 384))
+        chan = ids((256, 64), 0) // 4
+        diag = ids((256, 256), 0) % 4 == ids((256, 256), 1) // 64
+        for dst, sel in ((we_ref, chan == ids((256, 64), 1)), (wo_ref, chan == (ids((256, 64), 1) ^ 1))):
+            for n, w_ref in enumerate((wl_ref, wlg_ref, wr_ref, wrg_ref)):
+                t = pick(sel, w_ref[...])
+                t = jnp.concatenate([t] * 4, axis=1)
+                dst[256 * n:256 * n + 256, :] = jnp.where(diag, t, 0.0).astype(jnp.bfloat16)
+
+    gain = gain_ref[...][None]
+    low = ids((32, 8, 384), 1) < 4
     for half in range(2):
-        z = z_ref[16 * half:16 * half + 16].astype(jnp.float32)
-        x = norm_channels(z, gain, 1).astype(jnp.bfloat16).reshape(4, 256, 192)
-        m = m_ref[16 * half:16 * half + 16].astype(jnp.float32)
-
-        def lanes(p, q):
-            return jnp.concatenate([p[:, :128], q[:, :128], p[:, 128:], q[:, 128:]], axis=1)
-
         acts = []
         for par, w_ref in ((0, we_ref), (1, wo_ref)):
-            rhs = lanes(x[par], x[par + 2])
-            keep = lanes(m[4 * par:4 * par + 4], m[4 * par + 8:4 * par + 12])
+            r = 16 * half + 4 * par
+            z = lanes(z_ref[r:r + 4], z_ref[r + 8:r + 12]).astype(jnp.float32)
+            rhs = norm_channels(z, gain, 1).astype(jnp.bfloat16).reshape(256, 384)
+            keep = lanes(m_ref[r:r + 4].astype(jnp.float32), m_ref[r + 8:r + 12].astype(jnp.float32))
             keep = jnp.concatenate([keep, keep], axis=0)[None]
             proj = jnp.dot(w_ref[...], rhs, preferred_element_type=jnp.float32)
             proj = proj.reshape(4, 32, 8, 384)
             acts.append((keep * sigmoid(proj[1]) * proj[0], keep * sigmoid(proj[3]) * proj[2]))
-        low = lax.broadcasted_iota(jnp.int32, (32, 8, 384), 1) < 4
         for e, o, ref in ((acts[0][0], acts[1][0], a_ref), (acts[0][1], acts[1][1], b_ref)):
             first = jnp.where(low, e, o)
             second = jnp.where(low, o, e)
@@ -57,7 +79,7 @@
                 ref[:, sec, 8 * half:8 * half + 8, :] = both[:, :, 128 * sec:128 * sec + 128]
 
 
-def project(z, m, gin, w_even, w_odd):
+def project(z, m, gin, w_l, w_lg, w_r, w_rg):
     full = lambda i: (0, 0)
     tile = jax.ShapeDtypeStruct((64, 3, 96, 128), jnp.bfloat16)
     out_spec = pl.BlockSpec((64, 3, 16, 128), lambda i: (0, 0, i, 0))
@@ -68,13 +90,16 @@
         in_specs=[
             pl.BlockSpec((32, 64, 192), lambda i: (i, 0, 0)),
             pl.BlockSpec((32, 192), lambda i: (i, 0)),
-            pl.BlockSpec((64, 1), full),
-            pl.BlockSpec((1024, 256), full),
-            pl.BlockSpec((1024, 256), full),
+            pl.BlockSpec((1, 64), full),
+        ] + [pl.BlockSpec((64, 64), full)] * 4,
+        out_specs=[out_spec, out_spec],
+        scratch_shapes=[
+            pltpu.VMEM((64, 384), jnp.float32),
+            pltpu.VMEM((1024, 256), jnp.bfloat16),
+            pltpu.VMEM((1024, 256), jnp.bfloat16),
         ],
-        out_specs=[out_spec, out_spec],
         compiler_params=pltpu.CompilerParams(vmem_limit_bytes=60 * 1024 * 1024),
-    )(z, m, gin, w_even, w_odd)
+    )(z, m, gin, w_l, w_lg, w_r, w_rg)
 
 
 def channel_sum(pa, pb, h, buf, at):
@@ -232,6 +257,9 @@
     def in_range(s, lag):
         return (s >= lag) & (s < CHUNKS + lag)
 
+    b_lag = jnp.where(is_inner, INNER_LAG, B_LAG)
+    sum_lag = jnp.where(is_inner, INNER_LAG + 1, SUM_LAG)
+
     def step(s, _):
         @pl.when(s < CHUNKS)
         def _():
@@ -282,22 +310,22 @@
             wait_slot(pb, sem_b, across, c)
             e_far(c).start()
 
-        @pl.when(in_range(s, B_LAG) & not_edge)
-        def _():
-            c = s - B_LAG
+        @pl.when(in_range(s, b_lag) & not_edge)
+        def _():
+            c = s - b_lag
             wait_slot(pb, sem_b, across, c)
             b_relay(c).start()
 
-        for lag, r, n in ((EDGE_LAG, row, 15), (SHARE_LAG, across, 16)):
-            @pl.when(in_range(s, lag) & is_inner)
-            def _():
-                c = s - lag
+        for r, n in ((row, 15), (across, 16)):
+            @pl.when(in_range(s, INNER_LAG) & is_inner)
+            def _():
+                c = s - INNER_LAG
                 wait_slot(pe, sem_e, r, c)
                 e_share(r, n, c).start()
 
-        @pl.when(in_range(s, SUM_LAG) & not_edge)
-        def _():
-            c = s - SUM_LAG
+        @pl.when(in_range(s, sum_lag) & not_edge)
+        def _():
+            c = s - sum_lag
             for r in (partner, diagonal):
                 wait_slot(pb, sem_b, r, c)
             for kk in range(4):
@@ -333,7 +361,7 @@
             o_own(c).start()
         return 0
 
-    lax.fori_loop(0, CHUNKS + SUM_LAG, step, 0)
+    lax.fori_loop(0, CHUNKS + max(SUM_LAG, INNER_LAG + 1), step, 0)
 
     @pl.when(not_edge)
     def _():
@@ -413,53 +441,60 @@
     return o
 
 
-I_STEP = 16
-
-
-def finish_kernel(wide_ref, rest_ref, z_ref, gin_ref, gout_ref, wg_ref, wo_ref, out_ref):
-    upper = pl.program_id(0) >= 96 // I_STEP
-    for q in range(I_STEP // 8):
-        rest = rest_ref[:, 0, 8 * q:8 * q + 8, :]
-        rest = jnp.where(upper, rest[:, :, 64:], rest[:, :, :64])
-        o = jnp.concatenate([wide_ref[:, 0, 8 * q:8 * q + 8, :], rest], axis=2)
-        yv = norm_channels(o, gout_ref[...], 0).astype(jnp.bfloat16).reshape(512, 192)
-        upd = jnp.dot(wo_ref[...], yv, preferred_element_type=jnp.float32)
-        zv = z_ref[8 * q:8 * q + 8].astype(jnp.float32)
-        x = norm_channels(zv, gin_ref[...][None], 1).astype(jnp.bfloat16).reshape(2, 256, 192)
-        for s in range(2):
-            gate = sigmoid(jnp.dot(wg_ref[...], x[s], preferred_element_type=jnp.float32))
-            res = zv[4 * s:4 * s + 4].reshape(256, 192) + gate * upd[256 * s:256 * s + 256]
-            out_ref[8 * q + 4 * s:8 * q + 4 * s + 4] = res.astype(jnp.bfloat16).reshape(4, 64, 192)
-
-
-def finish(o, z, gin, gout, wg, wo):
-    rows = pl.BlockSpec((I_STEP, 64, 192), lambda i: (i, 0, 0))
-    full2 = lambda i: (0, 0)
-    half = 96 // I_STEP
-    return pl.pallas_call(
+def finish_kernel(o_ref, z_ref, gin_ref, gout_ref, wg_ref, wo_ref, out_ref, gi_ref, go_ref, wg4_ref, wo8_ref):
+    @pl.when(pl.program_id(0) == 0)
+    def _():
+        gi_ref[...] = jnp.broadcast_to(column(ids((64, 64), 0) == ids((64, 64), 1), gin_ref[...]), (64, 384))
+        go_ref[...] = jnp.broadcast_to(column(ids((512, 64), 0) // 8 == ids((512, 64), 1), gout_ref[...]), (512, 128))
+        t = pick(ids((256, 64), 0) % 64 == ids((256, 64), 1), wg_ref[...])
+        t = jnp.concatenate([t] * 4, axis=1)
+        same = ids((256, 256), 0) // 64 == ids((256, 256), 1) // 64
+        wg4_ref[...] = jnp.where(same, t, 0.0).astype(jnp.bfloat16)
+        t = pick(ids((512, 64), 0) % 64 == ids((512, 64), 1), wo_ref[...]).astype(jnp.bfloat16)
+        wide = (ids((64, 512), 1) // 8 == ids((64, 512), 0)).astype(jnp.bfloat16)
+        t = jnp.dot(t, wide, preferred_element_type=jnp.float32)
+        same = ids((512, 512), 0) // 64 == ids((512, 512), 1) % 8
+        wo8_ref[...] = jnp.where(same, t, 0.0).astype(jnp.bfloat16)
+
+    normed = []
+    for sec in range(3):
+        v = norm_channels(o_ref[:, sec], 1.0, 0).reshape(512, 128) * go_ref[...]
+        normed.append(v.astype(jnp.bfloat16))
+    upd = jnp.dot(wo8_ref[...], jnp.concatenate(normed, axis=1), preferred_element_type=jnp.float32)
+    z = lanes(z_ref[0], z_ref[1]).astype(jnp.float32)
+    x = norm_channels(z, gi_ref[...][None], 1).astype(jnp.bfloat16).reshape(512, 384)
+    gate = jnp.concatenate(
+        [jnp.dot(wg4_ref[...], x[256 * s:256 * s + 256], preferred_element_type=jnp.float32) for s in range(2)], axis=0)
+    res = (z.reshape(512, 384) + sigmoid(gate) * upd).astype(jnp.bfloat16).reshape(8, 64, 384)
+    out_ref[0] = jnp.concatenate([res[:, :, :128], res[:, :, 256:320]], axis=2)
+    out_ref[1] = jnp.concatenate([res[:, :, 128:256], res[:, :, 320:]], axis=2)
+
+
+def finish(o, z, gin, gout, w_g, w_o):
+    rows = pl.BlockSpec((2, 8, 64, 192), lambda i: (0, i, 0, 0))
+    full = lambda i: (0, 0)
+    out = pl.pallas_call(
         finish_kernel,
-        grid=(192 // I_STEP,),
-        out_shape=jax.ShapeDtypeStruct((192, 64, 192), jnp.bfloat16),
+        grid=(12,),
+        out_shape=jax.ShapeDtypeStruct((2, 96, 64, 192), jnp.bfloat16),
         in_specs=[
-            pl.BlockSpec((64, 1, I_STEP, 128), lambda i: (0, i // half, i % half, 0)),
-            pl.BlockSpec((64, 1, I_STEP, 128), lambda i: (0, 2, i % half, 0)),
+            pl.BlockSpec((64, 3, 8, 128), lambda i: (0, 0, i, 0)),
             rows,
-            pl.BlockSpec((64, 1), full2),
-            pl.BlockSpec((64, 1, 1), lambda i: (0, 0, 0)),
-            pl.BlockSpec((256, 256), full2),
-            pl.BlockSpec((512, 512), full2),
+            pl.BlockSpec((1, 64), full),
+            pl.BlockSpec((1, 64), full),
+            pl.BlockSpec((64, 64), full),
+            pl.BlockSpec((64, 64), full),
         ],
         out_specs=rows,
+        scratch_shapes=[
+            pltpu.VMEM((64, 384), jnp.float32),
+            pltpu.VMEM((512, 128), jnp.float32),
+            pltpu.VMEM((256, 256), jnp.bfloat16),
+            pltpu.VMEM((512, 512), jnp.bfloat16),
+        ],
         compiler_params=pltpu.CompilerParams(vmem_limit_bytes=60 * 1024 * 1024),
-    )(o, o, z, gin, gout, wg, wo)
-
-
-def spread(w, n, swap=False):
-    t = w.T
-    if swap:
-        t = t.reshape(32, 2, 64)[:, ::-1].reshape(64, 64)
-    eye = jnp.eye(n, dtype=w.dtype)
-    return (t[:, None, None, :] * eye[None, :, :, None]).reshape(64 * n, 64 * n)
+    )(o, z.reshape(2, 96, 64, 192), gin, gout, w_g, w_o)
+    return out.reshape(192, 64, 192)
 
 
 def solution(mesh):
@@ -469,16 +504,9 @@
 
     def local_step(pair, mask, gin, w_l, w_lg, w_r, w_rg, w_g, gout, w_o):
         z = jnp.transpose(pair, (0, 2, 1))
-        gin_c = gin.astype(jnp.float32)[:, None]
-        gout_c = gout.astype(jnp.float32)[:, None, None]
-        w_even = jnp.concatenate([spread(w, 4) for w in (w_l, w_lg, w_r, w_rg)], axis=0)
-        w_odd = jnp.concatenate([spread(w, 4, True) for w in (w_l, w_lg, w_r, w_rg)], axis=0)
-        eye4, eye8 = jnp.eye(4, dtype=w_g.dtype), jnp.eye(8, dtype=w_o.dtype)
-        wg4 = (eye4[:, None, :, None] * w_g.T[None, :, None, :]).reshape(256, 256)
-        wo8 = (eye8[:, None, None, :] * w_o.T[None, :, :, None]).reshape(512, 512)
-        a, b = project(z, mask, gin_c, w_even, w_odd)
+        a, b = project(z, mask, gin[None], w_l, w_lg, w_r, w_rg)
         o = move(a, b)
-        out = finish(o, z, gin_c, gout_c, wg4, wo8)
+        out = finish(o, z, gin[None], gout[None], w_g, w_o)
         return jnp.transpose(out, (0, 2, 1))
 
     return jax.shard_map(local_step, mesh=mesh, in_specs=(tile_spec, mask_spec) + (replicated,) * 8, out_specs=tile_spec, check_vma=False)

time: 370 us -> 346 us (0.935)
  local copies, waits for them, and re-layouts: 9.96 us -> 0 us
  Pallas kernels: 354 us -> 345 us
  other arithmetic: 4.3 us -> 0 us
    pallas_call x1, Pallas kernels: 321 us -> 315 us  [move(): pl.pallas_call(move_kernel, out_shape=[jax.ShapeDtypeStruct(tile, jnp.flo...]
    mul x11 -> x0, local copies, waits for them, and re-layouts: 4.17 us -> none  [the longest x8 1.71 us: spread(): return (t[:, None, None, :] * eye[None, :, :, None]).reshape(64 * n, 64 * n)]
where the time goes in v5:
time: 346 us; the launch traced here: 345 us
  Pallas kernels  345 us (100%)
    pallas_call x1, Pallas kernels, move(): pl.pallas_call(move_kernel, out_shape=[jax.ShapeDtypeStruct(tile, jnp.flo...  315 us
    pallas_call x1, Pallas kernels, finish(): pl.pallas_call(finish_kernel, grid=(12,), out_shape=jax.ShapeDtypeStruct(...  16.9 us
    pallas_call x1, Pallas kernels, project(): pl.pallas_call(project_kernel, grid=(6,), out_shape=[tile, tile], in_spec...  13.1 us

profile of v5, /device:TPU:16, one launch (start us, length us, event | category | flops | bytes accessed | tf_op | source)
XLA Modules:
  0.0 344.9 jit_solution(14715900975674339072)
XLA Ops:
  0.0 13.1 %shard_map.100 = (bf16[64,3,96,128]{3,2,1,0:T(8,128)(2,1)}, bf16[64,3,96,128]{3,2,1,0:T(8,128)(2,1)}) custom-call(bf16[192,64,192]{2,1,0:T(8,128)(2,1)} %bitcast.8, s32[192,192]{1,0:T(8,128)} %m_ref.1, bf16[1,64]{1,0:T(2,128)(2,1)} %bitcast.10, bf16[64,64]{1,0:T(8,128)(2,1)} %wl_ref.1, bf16[64,64]{1,0:T(8,128)(2,1)} %wlg_ref.1, bf16[64,64]{1,0:T(8,128)(2,1)} %wr_ref.1, ...), custom_call_target="tpu_custom_call" | custom-call | tf_op jit(solution)/shard_map/pallas_call | solution.py:86
  13.1 314.9 %shard_map.101 = (f32[64,3,96,128]{3,2,1,0:T(8,128)}, bf16[2,64,3,96,128]{4,3,2,1,0:T(8,128)(2,1)}) custom-call(bf16[64,3,96,128]{3,2,1,0:T(8,128)(2,1)} %get-tuple-element.8.a_ref, bf16[64,3,96,128]{3,2,1,0:T(8,128)(2,1)} %get-tuple-element.9.b_ref), custom_call_target="tpu_custom_call" | custom-call | tf_op jit(solution)/shard_map/pallas_call | solution.py:423
  328.0 16.9 %shard_map.102 = bf16[2,96,64,192]{3,2,1,0:T(8,128)(2,1)} custom-call(f32[64,3,96,128]{3,2,1,0:T(8,128)} %get-tuple-element.10.o_ref, bf16[2,96,64,192]{3,2,1,0:T(8,128)(2,1)} %bitcast.9, bf16[1,64]{1,0:T(2,128)(2,1)} %bitcast.11, bf16[1,64]{1,0:T(2,128)(2,1)} %bitcast.12, bf16[64,64]{1,0:T(8,128)(2,1)} %wg_ref.1, bf16[64,64]{1,0:T(8,128)(2,1)} %wo_ref.1), custom_call_target="tpu_custom_call" | custom-call | tf_op jit(solution)/shard_map/pallas_call | solution.py:476

commit v6 on v5

--- a/solution.py
+++ b/solution.py
@@ -8,15 +8,15 @@
 LN_EPS = 0.00001
 MESH = pl.DeviceIdType.MESH
 CHUNKS = 32
-NEAR_LAG = 1
-CROSS_LAG = 2
-HOP_LAG = 3
-PASS_LAG = 5
-WAY_LAG = 3
-B_LAG = 3
-EDGE_LAG = 3
-SUM_LAG = 9
-INNER_LAG = 7
+NEAR_LAG = 0
+CROSS_LAG = 1
+HOP_LAG = 1
+PASS_LAG = 2
+WAY_LAG = 1
+B_LAG = 1
+EDGE_LAG = 1
+SUM_LAG = 4
+INNER_LAG = 3
 
 
 def sigmoid(v):
@@ -261,26 +261,6 @@
     sum_lag = jnp.where(is_inner, INNER_LAG + 1, SUM_LAG)
 
     def step(s, _):
-        @pl.when(s < CHUNKS)
-        def _():
-            @pl.when(jnp.logical_not(own_home))
-            def _():
-                to_home(s).start()
-
-            @pl.when(sends_far)
-            def _():
-                to_way(s).start()
-
-            b_far(s).start()
-
-            @pl.when(is_edge)
-            def _():
-                e_own(s).start()
-
-            @pl.when(not_edge)
-            def _():
-                b_near(s).start()
-
         for lag, kk, who in forwards:
             @pl.when(in_range(s, lag) & who)
             def _():
@@ -294,6 +274,26 @@
                 @pl.when(goes_left[kk])
                 def _():
                     left(kk, c).start()
+
+        @pl.when(s < CHUNKS)
+        def _():
+            @pl.when(jnp.logical_not(own_home))
+            def _():
+                to_home(s).start()
+
+            @pl.when(sends_far)
+            def _():
+                to_way(s).start()
+
+            b_far(s).start()
+
+            @pl.when(is_edge)
+            def _():
+                e_own(s).start()
+
+            @pl.when(not_edge)
+            def _():
+                b_near(s).start()
 
         @pl.when(in_range(s, WAY_LAG))
         def _():

time: 346 us -> 329 us (0.951)
  Pallas kernels: 345 us -> 328 us
    pallas_call x1, Pallas kernels: 315 us -> 298 us  [move(): pl.pallas_call(move_kernel, out_shape=[jax.ShapeDtypeStruct(tile, jnp.flo...]
where the time goes in v6:
time: 329 us; the launch traced here: 328 us
  Pallas kernels  328 us (100%)
    pallas_call x1, Pallas kernels, move(): pl.pallas_call(move_kernel, out_shape=[jax.ShapeDtypeStruct(tile, jnp.flo...  298 us
    pallas_call x1, Pallas kernels, finish(): pl.pallas_call(finish_kernel, grid=(12,), out_shape=jax.ShapeDtypeStruct(...  16.9 us
    pallas_call x1, Pallas kernels, project(): pl.pallas_call(project_kernel, grid=(6,), out_shape=[tile, tile], in_spec...  13.1 us

profile of v6, /device:TPU:16, one launch (start us, length us, event | category | flops | bytes accessed | tf_op | source)
XLA Modules:
  0.0 328.2 jit_solution(17674499736637411351)
XLA Ops:
  0.0 13.1 %shard_map.100 = (bf16[64,3,96,128]{3,2,1,0:T(8,128)(2,1)}, bf16[64,3,96,128]{3,2,1,0:T(8,128)(2,1)}) custom-call(bf16[192,64,192]{2,1,0:T(8,128)(2,1)} %bitcast.8, s32[192,192]{1,0:T(8,128)} %m_ref.1, bf16[1,64]{1,0:T(2,128)(2,1)} %bitcast.10, bf16[64,64]{1,0:T(8,128)(2,1)} %wl_ref.1, bf16[64,64]{1,0:T(8,128)(2,1)} %wlg_ref.1, bf16[64,64]{1,0:T(8,128)(2,1)} %wr_ref.1, ...), custom_call_target="tpu_custom_call" | custom-call | tf_op jit(solution)/shard_map/pallas_call | solution.py:86
  13.1 298.2 %shard_map.101 = (f32[64,3,96,128]{3,2,1,0:T(8,128)}, bf16[2,64,3,96,128]{4,3,2,1,0:T(8,128)(2,1)}) custom-call(bf16[64,3,96,128]{3,2,1,0:T(8,128)(2,1)} %get-tuple-element.8.a_ref, bf16[64,3,96,128]{3,2,1,0:T(8,128)(2,1)} %get-tuple-element.9.b_ref), custom_call_target="tpu_custom_call" | custom-call | tf_op jit(solution)/shard_map/pallas_call | solution.py:423
  311.3 16.9 %shard_map.102 = bf16[2,96,64,192]{3,2,1,0:T(8,128)(2,1)} custom-call(f32[64,3,96,128]{3,2,1,0:T(8,128)} %get-tuple-element.10.o_ref, bf16[2,96,64,192]{3,2,1,0:T(8,128)(2,1)} %bitcast.9, bf16[1,64]{1,0:T(2,128)(2,1)} %bitcast.11, bf16[1,64]{1,0:T(2,128)(2,1)} %bitcast.12, bf16[64,64]{1,0:T(8,128)(2,1)} %wg_ref.1, bf16[64,64]{1,0:T(8,128)(2,1)} %wo_ref.1), custom_call_target="tpu_custom_call" | custom-call | tf_op jit(solution)/shard_map/pallas_call | solution.py:476

commit v7 on v6

--- a/solution.py
+++ b/solution.py
@@ -16,7 +16,7 @@
 B_LAG = 1
 EDGE_LAG = 1
 SUM_LAG = 4
-INNER_LAG = 3
+INNER_LAG = 2
 
 
 def sigmoid(v):
@@ -456,29 +456,31 @@
         same = ids((512, 512), 0) // 64 == ids((512, 512), 1) % 8
         wo8_ref[...] = jnp.where(same, t, 0.0).astype(jnp.bfloat16)
 
-    normed = []
-    for sec in range(3):
-        v = norm_channels(o_ref[:, sec], 1.0, 0).reshape(512, 128) * go_ref[...]
-        normed.append(v.astype(jnp.bfloat16))
-    upd = jnp.dot(wo8_ref[...], jnp.concatenate(normed, axis=1), preferred_element_type=jnp.float32)
-    z = lanes(z_ref[0], z_ref[1]).astype(jnp.float32)
-    x = norm_channels(z, gi_ref[...][None], 1).astype(jnp.bfloat16).reshape(512, 384)
-    gate = jnp.concatenate(
-        [jnp.dot(wg4_ref[...], x[256 * s:256 * s + 256], preferred_element_type=jnp.float32) for s in range(2)], axis=0)
-    res = (z.reshape(512, 384) + sigmoid(gate) * upd).astype(jnp.bfloat16).reshape(8, 64, 384)
-    out_ref[0] = jnp.concatenate([res[:, :, :128], res[:, :, 256:320]], axis=2)
-    out_ref[1] = jnp.concatenate([res[:, :, 128:256], res[:, :, 320:]], axis=2)
+    for q in range(2):
+        rows = slice(8 * q, 8 * q + 8)
+        normed = []
+        for sec in range(3):
+            v = norm_channels(o_ref[:, sec, rows], 1.0, 0).reshape(512, 128) * go_ref[...]
+            normed.append(v.astype(jnp.bfloat16))
+        upd = jnp.dot(wo8_ref[...], jnp.concatenate(normed, axis=1), preferred_element_type=jnp.float32)
+        z = lanes(z_ref[0, rows], z_ref[1, rows]).astype(jnp.float32)
+        x = norm_channels(z, gi_ref[...][None], 1).astype(jnp.bfloat16).reshape(512, 384)
+        gate = jnp.concatenate(
+            [jnp.dot(wg4_ref[...], x[256 * s:256 * s + 256], preferred_element_type=jnp.float32) for s in range(2)], axis=0)
+        res = (z.reshape(512, 384) + sigmoid(gate) * upd).astype(jnp.bfloat16).reshape(8, 64, 384)
+        out_ref[0, rows] = jnp.concatenate([res[:, :, :128], res[:, :, 256:320]], axis=2)
+        out_ref[1, rows] = jnp.concatenate([res[:, :, 128:256], res[:, :, 320:]], axis=2)
 
 
 def finish(o, z, gin, gout, w_g, w_o):
-    rows = pl.BlockSpec((2, 8, 64, 192), lambda i: (0, i, 0, 0))
+    rows = pl.BlockSpec((2, 16, 64, 192), lambda i: (0, i, 0, 0))
     full = lambda i: (0, 0)
     out = pl.pallas_call(
         finish_kernel,
-        grid=(12,),
+        grid=(6,),
         out_shape=jax.ShapeDtypeStruct((2, 96, 64, 192), jnp.bfloat16),
         in_specs=[
-            pl.BlockSpec((64, 3, 8, 128), lambda i: (0, 0, i, 0)),
+            pl.BlockSpec((64, 3, 16, 128), lambda i: (0, 0, i, 0)),
             rows,
             pl.BlockSpec((1, 64), full),
             pl.BlockSpec((1, 64), full),

time: 329 us -> 326 us (level)
  no operation moved by 1% of the time
where the time goes in v7:
time: 326 us; the launch traced here: 325 us
  Pallas kernels  325 us (100%)
    pallas_call x1, Pallas kernels, move(): pl.pallas_call(move_kernel, out_shape=[jax.ShapeDtypeStruct(tile, jnp.flo...  298 us
    pallas_call x1, Pallas kernels, finish(): pl.pallas_call(finish_kernel, grid=(6,), out_shape=jax.ShapeDtypeStruct((...  14.2 us
    pallas_call x1, Pallas kernels, project(): pl.pallas_call(project_kernel, grid=(6,), out_shape=[tile, tile], in_spec...  13.1 us

profile of v7, /device:TPU:16, one launch (start us, length us, event | category | flops | bytes accessed | tf_op | source)
XLA Modules:
  0.0 325.2 jit_solution(6268625963440119044)
XLA Ops:
  0.0 13.1 %shard_map.100 = (bf16[64,3,96,128]{3,2,1,0:T(8,128)(2,1)}, bf16[64,3,96,128]{3,2,1,0:T(8,128)(2,1)}) custom-call(bf16[192,64,192]{2,1,0:T(8,128)(2,1)} %bitcast.8, s32[192,192]{1,0:T(8,128)} %m_ref.1, bf16[1,64]{1,0:T(2,128)(2,1)} %bitcast.10, bf16[64,64]{1,0:T(8,128)(2,1)} %wl_ref.1, bf16[64,64]{1,0:T(8,128)(2,1)} %wlg_ref.1, bf16[64,64]{1,0:T(8,128)(2,1)} %wr_ref.1, ...), custom_call_target="tpu_custom_call" | custom-call | tf_op jit(solution)/shard_map/pallas_call | solution.py:86
  13.1 297.8 %shard_map.101 = (f32[64,3,96,128]{3,2,1,0:T(8,128)}, bf16[2,64,3,96,128]{4,3,2,1,0:T(8,128)(2,1)}) custom-call(bf16[64,3,96,128]{3,2,1,0:T(8,128)(2,1)} %get-tuple-element.8.a_ref, bf16[64,3,96,128]{3,2,1,0:T(8,128)(2,1)} %get-tuple-element.9.b_ref), custom_call_target="tpu_custom_call" | custom-call | tf_op jit(solution)/shard_map/pallas_call | solution.py:423
  311.0 14.2 %shard_map.102 = bf16[2,96,64,192]{3,2,1,0:T(8,128)(2,1)} custom-call(f32[64,3,96,128]{3,2,1,0:T(8,128)} %get-tuple-element.10.o_ref, bf16[2,96,64,192]{3,2,1,0:T(8,128)(2,1)} %bitcast.9, bf16[1,64]{1,0:T(2,128)(2,1)} %bitcast.11, bf16[1,64]{1,0:T(2,128)(2,1)} %bitcast.12, bf16[64,64]{1,0:T(8,128)(2,1)} %wg_ref.1, bf16[64,64]{1,0:T(8,128)(2,1)} %wo_ref.1), custom_call_target="tpu_custom_call" | custom-call | tf_op jit(solution)/shard_map/pallas_call | solution.py:478

commit v8 on v7

--- a/solution.py
+++ b/solution.py
@@ -13,9 +13,9 @@
 HOP_LAG = 1
 PASS_LAG = 2
 WAY_LAG = 1
-B_LAG = 1
+B_LAG = 3
 EDGE_LAG = 1
-SUM_LAG = 4
+SUM_LAG = 8
 INNER_LAG = 2
 
 

time: 326 us -> 338 us (1.037)
  Pallas kernels: 325 us -> 337 us
    pallas_call x1, Pallas kernels: 298 us -> 310 us  [move(): pl.pallas_call(move_kernel, out_shape=[jax.ShapeDtypeStruct(tile, jnp.flo...]
where the time goes in v8:
time: 338 us; the launch traced here: 337 us
  Pallas kernels  337 us (100%)
    pallas_call x1, Pallas kernels, move(): pl.pallas_call(move_kernel, out_shape=[jax.ShapeDtypeStruct(tile, jnp.flo...  310 us
    pallas_call x1, Pallas kernels, finish(): pl.pallas_call(finish_kernel, grid=(6,), out_shape=jax.ShapeDtypeStruct((...  14.2 us
    pallas_call x1, Pallas kernels, project(): pl.pallas_call(project_kernel, grid=(6,), out_shape=[tile, tile], in_spec...  13.1 us

profile of v8, /device:TPU:16, one launch (start us, length us, event | category | flops | bytes accessed | tf_op | source)
XLA Modules:
  0.0 337.4 jit_solution(5801925192945496862)
XLA Ops:
  0.0 13.1 %shard_map.100 = (bf16[64,3,96,128]{3,2,1,0:T(8,128)(2,1)}, bf16[64,3,96,128]{3,2,1,0:T(8,128)(2,1)}) custom-call(bf16[192,64,192]{2,1,0:T(8,128)(2,1)} %bitcast.8, s32[192,192]{1,0:T(8,128)} %m_ref.1, bf16[1,64]{1,0:T(2,128)(2,1)} %bitcast.10, bf16[64,64]{1,0:T(8,128)(2,1)} %wl_ref.1, bf16[64,64]{1,0:T(8,128)(2,1)} %wlg_ref.1, bf16[64,64]{1,0:T(8,128)(2,1)} %wr_ref.1, ...), custom_call_target="tpu_custom_call" | custom-call | tf_op jit(solution)/shard_map/pallas_call | solution.py:86
  13.1 310.1 %shard_map.101 = (f32[64,3,96,128]{3,2,1,0:T(8,128)}, bf16[2,64,3,96,128]{4,3,2,1,0:T(8,128)(2,1)}) custom-call(bf16[64,3,96,128]{3,2,1,0:T(8,128)(2,1)} %get-tuple-element.8.a_ref, bf16[64,3,96,128]{3,2,1,0:T(8,128)(2,1)} %get-tuple-element.9.b_ref), custom_call_target="tpu_custom_call" | custom-call | tf_op jit(solution)/shard_map/pallas_call | solution.py:423
  323.2 14.2 %shard_map.102 = bf16[2,96,64,192]{3,2,1,0:T(8,128)(2,1)} custom-call(f32[64,3,96,128]{3,2,1,0:T(8,128)} %get-tuple-element.10.o_ref, bf16[2,96,64,192]{3,2,1,0:T(8,128)(2,1)} %bitcast.9, bf16[1,64]{1,0:T(2,128)(2,1)} %bitcast.11, bf16[1,64]{1,0:T(2,128)(2,1)} %bitcast.12, bf16[64,64]{1,0:T(8,128)(2,1)} %wg_ref.1, bf16[64,64]{1,0:T(8,128)(2,1)} %wo_ref.1), custom_call_target="tpu_custom_call" | custom-call | tf_op jit(solution)/shard_map/pallas_call | solution.py:478
